TPU v7x, 8 devices: a whole 2x2x1 slice. The times are simulated.
8 devices in a mesh: sp: 8 (over z, y, x, core).
Axes of the slice: x: 2, y: 2, z: 1, core: 2. Of those that a mesh axis runs over, the one named last changes fastest.
Arguments:
- x_in: bfloat16 [2048, 2048], P('sp')
- positions: int32 [2048], P('sp')
- d_out: bfloat16 [2048, 2048], P('sp')
- norm1_gain: bfloat16 [2048], P('sp')
- norm2_gain: bfloat16 [2048], P('sp')
- w_q: bfloat16 [2048, 32, 64], P('sp')
- w_k: bfloat16 [2048, 4, 64], P('sp')
- w_v: bfloat16 [2048, 4, 64], P('sp')
- w_o: bfloat16 [32, 64, 2048], P('sp')
- w_gate: bfloat16 [2048, 5632], P('sp')
- w_up: bfloat16 [2048, 5632], P('sp')
- w_down: bfloat16 [5632, 2048], P('sp')
Outputs:
- output 1: bfloat16 [2048, 2048], P('sp')
- output 2: bfloat16 [2048, 2048], P('sp')
- output 3: float32 [2048], P('sp')
- output 4: float32 [2048], P('sp')
- output 5: float32 [2048, 32, 64], P('sp')
- output 6: float32 [2048, 4, 64], P('sp')
- output 7: float32 [2048, 4, 64], P('sp')
- output 8: float32 [32, 64, 2048], P('sp')
- output 9: float32 [2048, 5632], P('sp')
- output 10: float32 [2048, 5632], P('sp')
- output 11: float32 [5632, 2048], P('sp')
All inputs are finite; a program needn't handle non-finite values.
Results may differ from a plain program's by a relative error of at most 0.0187894.
Values are sent between devices in bfloat16 or wider.
A program may use at most 1 GiB of HBM per device.

v0:
```python
import functools
import jax
import jax.numpy as jnp
from jax import lax
from jax.sharding import PartitionSpec as P

ROPE_BASE = 10000.0
NORM_EPS = 1e-5
NEG_LARGE = -1e30


def norm_forward(hidden, gain_vec):
    inv_rms = lax.rsqrt(jnp.mean(hidden * hidden, axis=-1, keepdims=True) + NORM_EPS)
    return hidden * inv_rms * gain_vec


def rope_tables(positions, head_dim):
    half_dim = head_dim // 2
    inv_freq = 1.0 / (ROPE_BASE ** (jnp.arange(half_dim, dtype=jnp.float32) * (2.0 / head_dim)))
    angles = positions.astype(jnp.float32)[:, None] * inv_freq[None, :]
    return jnp.cos(angles)[:, None, :], jnp.sin(angles)[:, None, :]


def rotate(values_in, cos_tab, sin_tab):
    half_dim = values_in.shape[-1] // 2
    first_half = values_in[..., :half_dim].astype(jnp.float32)
    second_half = values_in[..., half_dim:].astype(jnp.float32)
    return jnp.concatenate([first_half * cos_tab - second_half * sin_tab, second_half * cos_tab + first_half * sin_tab], axis=-1)


def gated_unit(gate_pre, up_pre):
    return jax.nn.silu(gate_pre) * up_pre


def attention_forward(queries, keys_all, values_all):
    seq_len = queries.shape[0]
    score_scale = queries.shape[-1] ** -0.5
    scores = jnp.einsum('skgd,tkd->kgst', queries, keys_all, preferred_element_type=jnp.float32) * score_scale
    causal = jnp.arange(seq_len)[:, None] >= jnp.arange(seq_len)[None, :]
    attn_probs = jax.nn.softmax(jnp.where(causal, scores, NEG_LARGE), axis=-1)
    attn_out = jnp.einsum('kgst,tkd->skgd', attn_probs.astype(jnp.bfloat16), values_all, preferred_element_type=jnp.float32)
    return attn_out.astype(jnp.bfloat16), attn_probs


def attention_backward(queries, keys_all, values_all, attn_probs, d_attn):
    score_scale = queries.shape[-1] ** -0.5
    probs_b16 = attn_probs.astype(jnp.bfloat16)
    d_probs = jnp.einsum('skgd,tkd->kgst', d_attn, values_all, preferred_element_type=jnp.float32)
    d_probs = d_probs.astype(jnp.bfloat16).astype(jnp.float32)
    row_dot = jnp.sum(d_probs * attn_probs, axis=-1, keepdims=True)
    d_scores = (attn_probs * (d_probs - row_dot) * score_scale).astype(jnp.bfloat16)
    d_queries = jnp.einsum('kgst,tkd->skgd', d_scores, keys_all, preferred_element_type=jnp.float32)
    d_keys = jnp.einsum('kgst,skgd->tkd', d_scores, queries, preferred_element_type=jnp.float32)
    d_values = jnp.einsum('kgst,skgd->tkd', probs_b16, d_attn, preferred_element_type=jnp.float32)
    return d_queries.astype(jnp.bfloat16), d_keys.astype(jnp.bfloat16), d_values.astype(jnp.bfloat16)


def solution(mesh):
    n_devices = mesh.shape['sp']
    gather_rows = functools.partial(lax.all_gather, axis_name='sp', axis=0, tiled=True)
    scatter_rows = functools.partial(lax.psum_scatter, axis_name='sp', scatter_dimension=0, tiled=True)
    to_heads = functools.partial(lax.all_to_all, axis_name='sp', split_axis=1, concat_axis=0, tiled=True)
    to_tokens = functools.partial(lax.all_to_all, axis_name='sp', split_axis=0, concat_axis=1, tiled=True)

    def layer_step(x_in, positions, d_out, norm1_gain, norm2_gain, w_q, w_k, w_v, w_o, w_gate, w_up, w_down):
        g1_full, g2_full, wq_full, wk_full, wv_full, wo_full, gate_full, up_full, down_full = [gather_rows(shard_w) for shard_w in (norm1_gain, norm2_gain, w_q, w_k, w_v, w_o, w_gate, w_up, w_down)]
        tokens = x_in.shape[0]
        seq_len = tokens * n_devices
        head_dim = w_q.shape[2]
        kv_heads = w_k.shape[1]
        kv_repeat = max(1, n_devices // kv_heads)
        cos_tab, sin_tab = rope_tables(positions, head_dim)

        x_f32 = x_in.astype(jnp.float32)
        normed_pre, norm1_pull = jax.vjp(norm_forward, x_f32, g1_full.astype(jnp.float32))
        normed = normed_pre.astype(jnp.bfloat16)
        q_lin = jnp.einsum('td,dhe->the', normed, wq_full, preferred_element_type=jnp.float32).astype(jnp.bfloat16)
        k_lin = jnp.einsum('td,dhe->the', normed, wk_full, preferred_element_type=jnp.float32).astype(jnp.bfloat16)
        v_lin = jnp.einsum('td,dhe->the', normed, wv_full, preferred_element_type=jnp.float32).astype(jnp.bfloat16)
        q_rot = rotate(q_lin, cos_tab, sin_tab).astype(jnp.bfloat16)
        k_rot = rotate(k_lin, cos_tab, sin_tab).astype(jnp.bfloat16)
        q_seq = to_heads(q_rot)
        k_seq = to_heads(jnp.repeat(k_rot, kv_repeat, axis=1))
        v_seq = to_heads(jnp.repeat(v_lin, kv_repeat, axis=1))
        kv_local = k_seq.shape[1]
        q_grouped = q_seq.reshape(seq_len, kv_local, -1, head_dim)
        attn_seq, attn_probs = attention_forward(q_grouped, k_seq, v_seq)
        attn_tok = to_tokens(attn_seq.reshape(seq_len, -1, head_dim))
        attn_proj = jnp.einsum('the,hed->td', attn_tok, wo_full, preferred_element_type=jnp.float32)
        hidden = (x_f32 + attn_proj).astype(jnp.bfloat16)
        hidden_f32 = hidden.astype(jnp.float32)
        mlp_pre, norm2_pull = jax.vjp(norm_forward, hidden_f32, g2_full.astype(jnp.float32))
        mlp_in = mlp_pre.astype(jnp.bfloat16)
        gate_act = jnp.dot(mlp_in, gate_full, preferred_element_type=jnp.float32).astype(jnp.bfloat16)
        up_act = jnp.dot(mlp_in, up_full, preferred_element_type=jnp.float32).astype(jnp.bfloat16)
        glu_pre, glu_pull = jax.vjp(gated_unit, gate_act.astype(jnp.float32), up_act.astype(jnp.float32))
        glu_out = glu_pre.astype(jnp.bfloat16)
        y_out = (hidden_f32 + jnp.dot(glu_out, down_full, preferred_element_type=jnp.float32)).astype(jnp.bfloat16)

        wq_back, wk_back, wv_back, wo_back, gate_back, up_back, down_back = [gather_rows(shard_w) for shard_w in (w_q, w_k, w_v, w_o, w_gate, w_up, w_down)]
        d_down = jnp.einsum('tf,td->fd', glu_out, d_out, preferred_element_type=jnp.float32)
        d_glu = jnp.einsum('td,fd->tf', d_out, down_back, preferred_element_type=jnp.float32).astype(jnp.bfloat16)
        d_gate_f, d_up_f = glu_pull(d_glu.astype(jnp.float32))
        d_gate_act = d_gate_f.astype(jnp.bfloat16)
        d_up_act = d_up_f.astype(jnp.bfloat16)
        d_gate = jnp.einsum('td,tf->df', mlp_in, d_gate_act, preferred_element_type=jnp.float32)
        d_up = jnp.einsum('td,tf->df', mlp_in, d_up_act, preferred_element_type=jnp.float32)
        d_mlp_in = (jnp.einsum('tf,df->td', d_gate_act, gate_back, preferred_element_type=jnp.float32) + jnp.einsum('tf,df->td', d_up_act, up_back, preferred_element_type=jnp.float32)).astype(jnp.bfloat16)
        d_hidden_norm, d_g2 = norm2_pull(d_mlp_in.astype(jnp.float32))
        d_hidden = (d_out.astype(jnp.float32) + d_hidden_norm).astype(jnp.bfloat16)
        d_wo = jnp.einsum('the,td->hed', attn_tok, d_hidden, preferred_element_type=jnp.float32)
        d_attn_tok = jnp.einsum('td,hed->the', d_hidden, wo_back, preferred_element_type=jnp.float32).astype(jnp.bfloat16)
        d_attn_seq = to_heads(d_attn_tok).reshape(seq_len, kv_local, -1, head_dim)
        d_q_seq, d_k_seq, d_v_seq = attention_backward(q_grouped, k_seq, v_seq, attn_probs, d_attn_seq)
        d_q_rot = to_tokens(d_q_seq.reshape(seq_len, -1, head_dim))
        d_k_rot = jnp.sum(to_tokens(d_k_seq).reshape(tokens, kv_heads, kv_repeat, head_dim), axis=2, dtype=jnp.float32).astype(jnp.bfloat16)
        d_v_lin = jnp.sum(to_tokens(d_v_seq).reshape(tokens, kv_heads, kv_repeat, head_dim), axis=2, dtype=jnp.float32).astype(jnp.bfloat16)
        d_q_lin = rotate(d_q_rot, cos_tab, -sin_tab).astype(jnp.bfloat16)
        d_k_lin = rotate(d_k_rot, cos_tab, -sin_tab).astype(jnp.bfloat16)
        d_wq = jnp.einsum('td,the->dhe', normed, d_q_lin, preferred_element_type=jnp.float32)
        d_wk = jnp.einsum('td,the->dhe', normed, d_k_lin, preferred_element_type=jnp.float32)
        d_wv = jnp.einsum('td,the->dhe', normed, d_v_lin, preferred_element_type=jnp.float32)
        d_normed = (jnp.einsum('the,dhe->td', d_q_lin, wq_back, preferred_element_type=jnp.float32) + jnp.einsum('the,dhe->td', d_k_lin, wk_back, preferred_element_type=jnp.float32) + jnp.einsum('the,dhe->td', d_v_lin, wv_back, preferred_element_type=jnp.float32)).astype(jnp.bfloat16)
        d_x_norm, d_g1 = norm1_pull(d_normed.astype(jnp.float32))
        d_x = (d_hidden.astype(jnp.float32) + d_x_norm).astype(jnp.bfloat16)
        grad_parts = (d_g1, d_g2, d_wq, d_wk, d_wv, d_wo, d_gate, d_up, d_down)
        return (y_out, d_x) + tuple(scatter_rows(grad_part) for grad_part in grad_parts)

    all_rows = P('sp')
    return jax.shard_map(layer_step, mesh=mesh, in_specs=(all_rows,) * 12, out_specs=(all_rows,) * 11, check_vma=False)
```

profile of v0, /device:TPU:0, one launch (start us, length us, event | category | flops | bytes accessed | tf_op | source)
XLA Modules:
  0.0 1783.8 jit_solution(13959194424041035666)
XLA Ops:
  35.1 16.1 all-gather.12.cloned.1.call-done
  53.2 49.9 %all-gather.14.cloned.1.call-done = bf16[2048,32,64]{0,2,1:T(8,128)(2,1)} async-done(((bf16[256,32,64]{0,2,1:T(8,128)(2,1)}), bf16[2048,32,64]{0,2,1:T(8,128)(2,1)}) %all-gather.14.cloned.1.call-update) | async-done | bytes 8388624 | tf_op jit(solution)/shard_map/all_gather | solution.py:66
  129.3 17.8 all-to-all-done.2
  147.2 26.0 %fusion.8 = (f32[4,2048]{1,0:T(4,128)S(1)}, f32[2048,2048,4]{1,0,2:T(8,128)}) fusion(pred[2048,2048]{0,1:T(8,128)(4,1)} %iota_compare_fusion, bf16[2048,64,1]{0,1,2:T(8,128)(2,1)S(1)} %reshape.246, bf16[2048,4,64]{0,2,1:T(8,128)(2,1)S(1)} %bitcast.227), kind=kOutput, calls=%fused_computation.11 | convolution fusion | flops 2197807104 | bytes 72646656 | tf_op jit(solution)/shard_map/skgd,tkd->kgst/dot_general | solution.py:38
  173.3 22.9 %fusion.7 = f32[4,2048]{1,0:T(4,128)S(1)} fusion(f32[2048,2048,4]{1,0,2:T(8,128)} %get-tuple-element.31, f32[4,2048]{1,0:T(4,128)S(1)} %get-tuple-element.30, pred[2048,2048]{0,1:T(8,128)(4,1)} %iota_compare_fusion), kind=kLoop, calls=%fused_computation.10 | loop fusion | flops 67100672 | bytes 71368704 | tf_op jit(solution)/shard_map/reduce_sum | solution.py:40
  196.3 27.8 %fusion.37 = bf16[2048,4,64]{0,2,1:T(8,128)(2,1)S(1)} fusion(bf16[2048,64,1]{0,1,2:T(8,128)(2,1)S(1)} %reshape.247, f32[4,2048]{1,0:T(4,128)S(1)} %fusion.7, f32[4,2048]{1,0:T(4,128)S(1)} %get-tuple-element.30, f32[2048,2048,4]{1,0,2:T(8,128)} %get-tuple-element.31, pred[2048,2048]{0,1:T(8,128)(4,1)} %iota_compare_fusion), kind=kOutput, calls=%fused_computation.71 | convolution fusion | flops 2231894016 | bytes 72679424 | tf_op jit(solution)/shard_map/kgst,tkd->skgd/dot_general | solution.py:41
  230.5 31.1 %all-gather.1 = bf16[8,1,256]{2,1,0:T(2,128)(2,1)S(1)} all-gather(bf16[1,1,256]{2,1,0:T(2,128)(2,1)S(1)} %reshape.236), channel_id=1, replica_groups=mesh['sp'=8] {'sp'}, dimensions={0}, use_global_device_ids=true | all-gather | bytes 4608 | tf_op jit(solution)/shard_map/all_gather | solution.py:66
  299.3 99.8 %all-gather.20.cloned.1.call-done = bf16[2048,5632]{1,0:T(8,128)(2,1)} async-done(((bf16[256,5632]{1,0:T(8,128)(2,1)}), bf16[2048,5632]{1,0:T(8,128)(2,1)}) %all-gather.20.cloned.1.call-update) | async-done | bytes 23068688 | tf_op jit(solution)/shard_map/all_gather | solution.py:66
  412.4 99.4 %all-gather.18.cloned.1.call-done = bf16[2048,5632]{1,0:T(8,128)(2,1)} async-done(((bf16[256,5632]{1,0:T(8,128)(2,1)}), bf16[2048,5632]{1,0:T(8,128)(2,1)}) %all-gather.18.cloned.1.call-update) | async-done | bytes 23068688 | tf_op jit(solution)/shard_map/all_gather | solution.py:66
  511.7 18.7 %fusion.22 = (bf16[256,5632]{1,0:T(8,128)(2,1)S(1)}, bf16[256,5632]{1,0:T(8,128)(2,1)}) fusion(f32[256,5632]{1,0:T(8,128)} %fusion.16, f32[256,5632]{1,0:T(8,128)} %fusion.15, bf16[2048,5632]{1,0:T(8,128)(2,1)} %all-gather.18.cloned.1.call-done, bf16[256,2048]{1,0:T(8,128)(2,1)S(1)} %get-tuple-element.33, f32[2048]{0:T(1024)S(1)} %bitcast.245, ...), kind=kOutput, calls=%fused_computation.34 | convolution fusion | flops 5926420480 | bytes 41427968 | tf_op jit(solution)/shard_map/dot_general | solution.py:94
  565.2 17.0 all_to_all.126
  582.4 39.9 %fusion.2 = (f32[4,2048]{1,0:T(4,128)S(1)}, bf16[2048,2048,4]{1,0,2:T(8,128)(2,1)}) fusion(f32[4,2048]{1,0:T(4,128)S(1)} %fusion.7, f32[4,2048]{1,0:T(4,128)S(1)} %get-tuple-element.30, f32[2048,2048,4]{1,0,2:T(8,128)} %get-tuple-element.31, pred[2048,2048]{0,1:T(8,128)(4,1)S(1)} %copy-done.3, bf16[2048,64,1]{0,1,2:T(8,128)(2,1)S(1)} %copy-done.35, ...), kind=kOutput, calls=%fused_computation.4 | convolution fusion | flops 2281693184 | bytes 106266624 | tf_op jit(solution)/shard_map/skgd,tkd->kgst/dot_general | solution.py:48
  622.3 44.1 %fusion.9 = bf16[4,2048,2048]{1,2,0:T(8,128)(2,1)} fusion(bf16[2048,2048,4]{1,0,2:T(8,128)(2,1)} %get-tuple-element.38, f32[4,2048]{1,0:T(4,128)S(1)} %get-tuple-element.37, f32[4,2048]{1,0:T(4,128)S(1)} %fusion.7, f32[4,2048]{1,0:T(4,128)S(1)} %get-tuple-element.30, f32[2048,2048,4]{1,0,2:T(8,128)} %get-tuple-element.31, pred[2048,2048]{0,1:T(8,128)(4,1)S(1)} %copy-done.3), kind=kLoop, calls=%fused_computation.12 | loop fusion | flops 150994944 | bytes 138510336 | tf_op jit(solution)/shard_map/reshape.28
  666.4 14.9 fusion.50
  695.9 27.6 %fusion.47 = bf16[2048,1,64]{0,2,1:T(8,128)(2,1)S(1)} fusion(bf16[2048,4,64]{0,2,1:T(8,128)(2,1)S(1)} %bitcast.238, f32[4,2048]{1,0:T(4,128)} %copy-done.37, f32[4,2048]{1,0:T(4,128)} %copy-done.36, f32[2048,2048,4]{1,0,2:T(8,128)} %get-tuple-element.31, pred[2048,2048]{0,1:T(8,128)(4,1)} %iota_compare_fusion), kind=kOutput, calls=%fused_computation.76 | convolution fusion | flops 2231500800 | bytes 72679424 | tf_op jit(solution)/shard_map/kgst,skgd->tkd/dot_general | solution.py:54
  774.5 17.1 all_to_all.129
  808.1 19.7 %fusion.88 = f32[2048,5632]{1,0:T(8,128)} fusion(bf16[256,5632]{1,0:T(8,128)(2,1)} %copy-done.14, bf16[256,2048]{1,0:T(8,128)(2,1)S(1)} %copy-done.7, f32[2048]{0:T(1024)S(1)} %bitcast.248, f32[256]{0:T(256)S(1)} %copy-done.39), kind=kOutput, calls=%fused_computation.142 | convolution fusion | flops 5907677184 | bytes 50078720 | tf_op jit(solution)/shard_map/td,tf->df/dot_general | solution.py:106
  827.9 21.5 %fusion.86 = f32[2048,5632]{1,0:T(8,128)} fusion(bf16[256,2048]{1,0:T(8,128)(2,1)S(1)} %copy-done.7, f32[2048]{0:T(1024)S(1)} %bitcast.249, f32[256]{0:T(256)S(1)} %copy-done.39, f32[256,5632]{1,0:T(8,128)} %fusion.16, bf16[256,5632]{1,0:T(8,128)(2,1)} %get-tuple-element.35), kind=kOutput, calls=%fused_computation.141 | convolution fusion | flops 5917769728 | bytes 55845888 | tf_op jit(solution)/shard_map/td,tf->df/dot_general | solution.py:107
  849.5 20.7 %fusion.104 = f32[5632,2048]{1,0:T(8,128)} fusion(bf16[256,2048]{1,0:T(8,128)(2,1)} %param.14, f32[256,5632]{1,0:T(8,128)} %fusion.15, bf16[256,5632]{1,0:T(8,128)(2,1)} %get-tuple-element.35), kind=kOutput, calls=%fused_computation.149 | convolution fusion | flops 5915672576 | bytes 55836672 | tf_op jit(solution)/shard_map/tf,td->fd/dot_general | solution.py:101
  892.1 22.4 %all-reduce.2 = (f32[2048]{0:T(1024)S(1)}, f32[2048]{0:T(1024)S(1)}) all-reduce(f32[2048]{0:T(1024)S(1)} %get-tuple-element.13, f32[2048]{0:T(1024)S(1)} %copy-done.44), channel_id=2, replica_groups=mesh['sp'=8] {'sp'}, use_global_device_ids=true, to_apply=%region_10.11.clone | all-reduce | flops 4096 | bytes 32768
  917.5 81.8 %reduce-scatter.8.cloned.1.call-done = f32[256,32,64]{0,2,1:T(8,128)} async-done(((f32[2048,32,64]{0,2,1:T(8,128)}), f32[256,32,64]{0,2,1:T(8,128)}) %reduce-scatter.8.cloned.1.call-update) | async-done | bytes 2097168 | tf_op jit(solution)/shard_map/reduce_scatter | solution.py:127
  999.3 259.1 %reduce-scatter.16.cloned.1.call-done = f32[256,5632]{1,0:T(8,128)} async-done(((f32[2048,5632]{1,0:T(8,128)}), f32[256,5632]{1,0:T(8,128)}) %reduce-scatter.16.cloned.1.call-update) | async-done | bytes 5767184 | tf_op jit(solution)/shard_map/reduce_scatter | solution.py:127
  1258.4 259.3 %reduce-scatter.18.cloned.1.call-done = f32[256,5632]{1,0:T(8,128)} async-done(((f32[2048,5632]{1,0:T(8,128)}), f32[256,5632]{1,0:T(8,128)}) %reduce-scatter.18.cloned.1.call-update) | async-done | bytes 5767184 | tf_op jit(solution)/shard_map/reduce_scatter | solution.py:127
  1517.7 259.1 %reduce-scatter.20.cloned.1.call-done = f32[704,2048]{1,0:T(8,128)} async-done(((f32[5632,2048]{1,0:T(8,128)}), f32[704,2048]{1,0:T(8,128)}) %reduce-scatter.20.cloned.1.call-update) | async-done | bytes 5767184 | tf_op jit(solution)/shard_map/reduce_scatter | solution.py:127
  (221 shorter events, 254.7 us)
Async XLA Ops:
  7.2 23.2 %all-gather.10.cloned.1.call-start = ((), (), s32[]{:S(2)}) async-start(), calls=%async_computation.15 | async-start | bytes 1179648 | tf_op jit(solution)/shard_map/all_gather | solution.py:66
  7.9 43.3 %all-gather.12.cloned.1.call-start = ((), (), s32[]{:S(2)}) async-start(), calls=%async_computation.16 | async-start | bytes 1179648 | tf_op jit(solution)/shard_map/all_gather | solution.py:66
  8.7 94.4 %all-gather.14.cloned.1.call-start = ((), (), s32[]{:S(2)}) async-start(), calls=%async_computation.17 | async-start | bytes 9437184 | tf_op jit(solution)/shard_map/all_gather | solution.py:66
  9.4 257.7 %all-gather.16.cloned.1.call-start = ((), (), s32[]{:S(2)}) async-start(), calls=%async_computation.18 | async-start | bytes 9437184 | tf_op jit(solution)/shard_map/all_gather | solution.py:66
  10.0 276.7 %all-gather.22.cloned.1.call-start = ((), (), s32[]{:S(2)}) async-start(), calls=%async_computation.21 | async-start | bytes 25952256 | tf_op jit(solution)/shard_map/all_gather | solution.py:66
  10.6 388.5 %all-gather.20.cloned.1.call-start = ((), (), s32[]{:S(2)}) async-start(), calls=%async_computation.20 | async-start | bytes 25952256 | tf_op jit(solution)/shard_map/all_gather | solution.py:66
  11.2 500.6 %all-gather.18.cloned.1.call-start = ((), (), s32[]{:S(2)}) async-start(), calls=%async_computation.19 | async-start | bytes 25952256 | tf_op jit(solution)/shard_map/all_gather | solution.py:66
  26.7 85.2 %copy-start.21 = (f32[256,32]{0,1:T(8,128)}, f32[256,32]{0,1:T(8,128)S(1)}, u32[]{:S(2)}) copy-start(f32[256,32]{0,1:T(8,128)S(1)} %get-tuple-element.29) | copy-start | bytes 98308
  33.0 76.1 %all-to-all-start = ((bf16[256,8,64]{0,2,1:T(8,128)(2,1)}), bf16[256,8,64]{0,2,1:T(8,128)(2,1)S(1)}, u32[]{:S(2)}, u32[]{:S(2)}) async-start(bf16[256,8,64]{0,2,1:T(8,128)(2,1)} %bitcast.3), calls=%async_computation | async-start | bytes 524288 | tf_op jit(solution)/shard_map/all_to_all | solution.py:84
  109.8 12.0 all-to-all-start.1
  121.8 25.3 %all-to-all-start.2 = ((bf16[256,32,64]{0,2,1:T(8,128)(2,1)}), bf16[256,32,64]{0,2,1:T(8,128)(2,1)S(1)}, u32[]{:S(2)}, u32[]{:S(2)}) async-start(bf16[256,32,64]{0,2,1:T(8,128)(2,1)} %pad_maximum_fusion), calls=%async_computation.2 | async-start | bytes 2097152 | tf_op jit(solution)/shard_map/all_to_all | solution.py:82
  173.3 449.0 %copy-start.36 = (f32[4,2048]{1,0:T(4,128)}, f32[4,2048]{1,0:T(4,128)S(1)}, u32[]{:S(2)}) copy-start(f32[4,2048]{1,0:T(4,128)S(1)} %get-tuple-element.30) | copy-start | bytes 98308
  196.3 426.1 %copy-start.37 = (f32[4,2048]{1,0:T(4,128)}, f32[4,2048]{1,0:T(4,128)S(1)}, u32[]{:S(2)}) copy-start(f32[4,2048]{1,0:T(4,128)S(1)} %fusion.7) | copy-start | bytes 98308
  228.1 33.5 %all-to-all-start.3 = ((bf16[8,2,32768]{2,1,0:T(2,128)(2,1)}), bf16[8,2,32768]{2,1,0:T(2,128)(2,1)S(1)}, u32[]{:S(2)}, u32[]{:S(2)}) async-start(bf16[8,2,32768]{2,1,0:T(2,128)(2,1)} %reshape.263), calls=%async_computation.3 | async-start | bytes 2097152 | tf_op jit(solution)/shard_map/all_to_all | solution.py:88
  230.4 687.1 %reduce-scatter.10.cloned.1.call-start = ((), (), s32[]{:S(2)}) async-start(), calls=%async_computation.23 | async-start | bytes 2359296 | tf_op jit(solution)/shard_map/reduce_scatter | solution.py:127
  261.6 296.6 %copy-start.24 = (f32[8,1,256]{2,1,0:T(1,128)}, f32[8,1,256]{2,1,0:T(1,128)S(1)}, u32[]{:S(2)}) copy-start(f32[8,1,256]{2,1,0:T(1,128)S(1)} %convert_element_type.238) | copy-start | bytes 24580
  273.3 284.9 %copy-start.6 = (bf16[256,2048]{1,0:T(8,128)(2,1)}, bf16[256,2048]{1,0:T(8,128)(2,1)S(1)}, u32[]{:S(2)}) copy-start(bf16[256,2048]{1,0:T(8,128)(2,1)S(1)} %get-tuple-element.33) | copy-start | bytes 3145732
  273.4 284.9 %copy-start.38 = (f32[256]{0:T(256)}, f32[256]{0:T(256)S(1)}, u32[]{:S(2)}) copy-start(f32[256]{0:T(256)S(1)} %fusion.84) | copy-start | bytes 3076
  695.9 221.7 %reduce-scatter.12.cloned.1.call-start = ((), (), s32[]{:S(2)}) async-start(), calls=%async_computation.24 | async-start | bytes 2359296 | tf_op jit(solution)/shard_map/reduce_scatter | solution.py:127
  745.5 172.0 %reduce-scatter.14.cloned.1.call-start = ((), (), s32[]{:S(2)}) async-start(), calls=%async_computation.25 | async-start | bytes 18874368 | tf_op jit(solution)/shard_map/reduce_scatter | solution.py:127
  753.8 245.5 %reduce-scatter.8.cloned.1.call-start = ((), (), s32[]{:S(2)}) async-start(), calls=%async_computation.22 | async-start | bytes 18874368 | tf_op jit(solution)/shard_map/reduce_scatter | solution.py:127
  806.9 451.5 %reduce-scatter.16.cloned.1.call-start = ((), (), s32[]{:S(2)}) async-start(), calls=%async_computation.26 | async-start | bytes 51904512 | tf_op jit(solution)/shard_map/reduce_scatter | solution.py:127
  827.8 689.9 %reduce-scatter.18.cloned.1.call-start = ((), (), s32[]{:S(2)}) async-start(), calls=%async_computation.27 | async-start | bytes 51904512 | tf_op jit(solution)/shard_map/reduce_scatter | solution.py:127
  849.4 927.4 %reduce-scatter.20.cloned.1.call-start = ((), (), s32[]{:S(2)}) async-start(), calls=%async_computation.28 | async-start | bytes 51904512 | tf_op jit(solution)/shard_map/reduce_scatter | solution.py:127
  (42 other events, 879.5 us)
Sparse Core Ops, SparseCore 0:
  9.8 20.5 all-gather.9
  32.2 18.9 all-gather.11
  53.1 49.9 all-gather.13
  104.7 58.1 all-gather.15
  164.5 122.1 all-gather.21
  288.4 110.7 all-gather.19
  400.9 110.7 all-gather.17
  696.0 31.6 reduce-scatter.9
  745.7 31.6 reduce-scatter.11
  781.3 106.9 reduce-scatter.13
  892.4 106.9 reduce-scatter.7
  1003.3 255.0 reduce-scatter.15
  1262.6 255.1 reduce-scatter.17
  1521.7 255.0 reduce-scatter.19
where the time goes:
time: 1790 us; the launch traced here: 1780 us
  waiting for transfers between devices  1170 us (65%)
  matrix products  348 us (19%)
  blocking collectives  118 us (7%)
  other arithmetic  81.1 us (5%)
  local copies, waits for them, and re-layouts  38.9 us (2%)
    reduce_scatter x7, waiting for transfers between devices, layer_step(): scatter_rows(grad_part)  859 us
    all_gather x7, waiting for transfers between devices, layer_step(): gather_rows(shard_w)  282 us
    another operation x5, other arithmetic  46.1 us
    all_gather x2, blocking collectives, layer_step(): gather_rows(shard_w)  44.7 us
    dot_general x1, matrix products, attention_backward(): jnp.einsum('skgd,tkd->kgst', d_attn, values_all, preferred_element_type=j...  39.9 us
  transfers between devices with their start and end apart: 18, of which 12 were waited for; matrix products, arithmetic and copies ran while one was open for 17% of the time, Pallas kernels for 0%

commit v1 on v0

v1 whole, which is shorter than its diff:
```python
import functools
import jax
import jax.numpy as jnp
from jax import lax
from jax.experimental import pallas as pl
from jax.experimental.pallas import tpu as pltpu
from jax.experimental.layout import Layout, with_layout_constraint
from jax.sharding import PartitionSpec as P

ROPE_BASE = 10000.0
NORM_EPS = 1e-5
NEG_LARGE = -1e30
BLOCK = 256
XOR_ORDER = (2, 4, 6, 3, 5, 7, 1)
B16 = jnp.bfloat16
F32 = jnp.float32


def inverse_rms(hidden):
    return lax.rsqrt(jnp.mean(hidden * hidden, axis=-1, keepdims=True) + NORM_EPS)


def rope_tables(positions, head_dim):
    half_dim = head_dim // 2
    inv_freq = 1.0 / (ROPE_BASE ** (jnp.arange(half_dim, dtype=F32) * (2.0 / head_dim)))
    angles = positions.astype(F32)[:, None] * inv_freq[None, :]
    return jnp.cos(angles)[:, None, :], jnp.sin(angles)[:, None, :]


def gated_unit(gate_pre, up_pre):
    return jax.nn.silu(gate_pre) * up_pre


def norm_backward(d_normed, hidden, inv_rms, gain):
    scaled = d_normed * gain
    row_dot = jnp.mean(scaled * hidden, axis=-1, keepdims=True)
    return inv_rms * scaled - hidden * (inv_rms * inv_rms * inv_rms * row_dot)


def stack_heads(block, heads, head_dim):
    return jnp.concatenate([block[:, h * head_dim:(h + 1) * head_dim] for h in range(heads)], axis=0)


def unstack_heads(rows, heads):
    size = rows.shape[0] // heads
    return jnp.concatenate([rows[h * size:(h + 1) * size] for h in range(heads)], axis=1)


def dot_f32(lhs, rhs, dims):
    return lax.dot_general(lhs, rhs, (dims, ((), ())), preferred_element_type=F32)


def causal_block(heads):
    shape = (heads * BLOCK, BLOCK)
    row = lax.broadcasted_iota(jnp.int32, shape, 0) % BLOCK
    col = lax.broadcasted_iota(jnp.int32, shape, 1)
    return row >= col


def attention_forward_kernel(heads, head_dim, scale, q_ref, k_ref, v_ref, o_ref, max_ref, inv_ref, score_ref, acc_ref):
    step = pl.program_id(0)
    queries = stack_heads(q_ref[...], heads, head_dim)
    last = pl.multiple_of(step * BLOCK, BLOCK)

    def scores_at(start):
        return dot_f32(queries, k_ref[pl.ds(start, BLOCK), :], ((1,), (1,))) * scale

    def fold(op, block):
        return op(block[:, :128], block[:, 128:])

    diag = jnp.where(causal_block(heads), scores_at(last), NEG_LARGE)
    score_ref[:, pl.ds(last, BLOCK)] = diag
    acc_ref[...] = fold(jnp.maximum, diag)

    @pl.loop(0, step)
    def _(j):
        start = pl.multiple_of(j * BLOCK, BLOCK)
        block = scores_at(start)
        score_ref[:, pl.ds(start, BLOCK)] = block
        acc_ref[...] = jnp.maximum(acc_ref[...], fold(jnp.maximum, block))

    row_max = jnp.max(acc_ref[...], axis=1, keepdims=True)
    max_ref[...] = row_max
    acc_ref[...] = jnp.zeros_like(acc_ref)

    @pl.loop(0, step + 1)
    def _(j):
        start = pl.multiple_of(j * BLOCK, BLOCK)
        block = jnp.exp(score_ref[:, pl.ds(start, BLOCK)] - row_max)
        score_ref[:, pl.ds(start, BLOCK)] = block
        acc_ref[...] += fold(jnp.add, block)

    inv_sum = 1.0 / jnp.sum(acc_ref[...], axis=1, keepdims=True)
    inv_ref[...] = inv_sum

    def weighted(j, total):
        start = pl.multiple_of(j * BLOCK, BLOCK)
        probs = (score_ref[:, pl.ds(start, BLOCK)] * inv_sum).astype(B16)
        return total + dot_f32(probs, v_ref[pl.ds(start, BLOCK), :], ((1,), (0,)))

    total = lax.fori_loop(0, step + 1, weighted, jnp.zeros((heads * BLOCK, head_dim), F32))
    o_ref[...] = unstack_heads(total.astype(B16), heads)


def attention_forward(q_rot, k_rot, v_lin, heads):
    seq_len, width = q_rot.shape
    head_dim = width // heads
    rows = heads * BLOCK
    steps = seq_len // BLOCK
    whole = pl.BlockSpec((seq_len, head_dim), lambda i: (0, 0))
    tokens = pl.BlockSpec((BLOCK, width), lambda i: (i, 0))
    stats = pl.BlockSpec((rows, 1), lambda i: (i, 0))
    stat_shape = jax.ShapeDtypeStruct((steps * rows, 1), F32)
    return pl.pallas_call(
        functools.partial(attention_forward_kernel, heads, head_dim, head_dim ** -0.5),
        grid=(steps,),
        out_shape=(jax.ShapeDtypeStruct((seq_len, width), B16), stat_shape, stat_shape),
        in_specs=[tokens, whole, whole],
        out_specs=(tokens, stats, stats),
        scratch_shapes=[pltpu.VMEM((rows, seq_len), F32), pltpu.VMEM((rows, 128), F32)],
        compiler_params=pltpu.CompilerParams(vmem_limit_bytes=48 * 1024 * 1024),
        cost_estimate=pl.CostEstimate(flops=20_000_000_000, bytes_accessed=4_000_000, transcendentals=8_000_000),
        name='attention_forward',
    )(q_rot, k_rot, v_lin)


def attention_backward_kernel(heads, head_dim, scale, q_ref, do_ref, k_ref, v_ref, max_ref, inv_ref, cos_ref, sin_ref, dq_ref, dk_ref, dv_ref, prob_ref, dp_ref, acc_ref, dk_acc, dv_acc):
    step = pl.program_id(0)
    queries = stack_heads(q_ref[...], heads, head_dim)
    d_out = stack_heads(do_ref[...], heads, head_dim)
    row_max = max_ref[...]
    inv_sum = inv_ref[...]
    last = pl.multiple_of(step * BLOCK, BLOCK)

    @pl.when(step == 0)
    def _():
        dk_acc[...] = jnp.zeros_like(dk_acc)
        dv_acc[...] = jnp.zeros_like(dv_acc)

    def scores_at(start):
        return dot_f32(queries, k_ref[pl.ds(start, BLOCK), :], ((1,), (1,))) * scale

    def first_pass(start, scores):
        probs = jnp.exp(scores - row_max) * inv_sum
        d_probs = dot_f32(d_out, v_ref[pl.ds(start, BLOCK), :], ((1,), (1,))).astype(B16)
        prob_ref[:, pl.ds(start, BLOCK)] = probs
        dp_ref[:, pl.ds(start, BLOCK)] = d_probs
        product = probs * d_probs.astype(F32)
        dv_acc[:, pl.ds(start, BLOCK)] += dot_f32(d_out, probs.astype(B16), ((0,), (0,)))
        return product[:, :128] + product[:, 128:]

    acc_ref[...] = first_pass(last, jnp.where(causal_block(heads), scores_at(last), NEG_LARGE))

    @pl.loop(0, step)
    def _(j):
        start = pl.multiple_of(j * BLOCK, BLOCK)
        acc_ref[...] += first_pass(start, scores_at(start))

    row_dot = jnp.sum(acc_ref[...], axis=1, keepdims=True)

    def second_pass(j, total):
        start = pl.multiple_of(j * BLOCK, BLOCK)
        at = pl.ds(start, BLOCK)
        d_scores = (prob_ref[:, at] * (dp_ref[:, at].astype(F32) - row_dot) * scale).astype(B16)
        dk_acc[:, at] += dot_f32(queries, d_scores, ((0,), (0,)))
        return total + dot_f32(d_scores, k_ref[at, :], ((1,), (0,)))

    total = lax.fori_loop(0, step + 1, second_pass, jnp.zeros((heads * BLOCK, head_dim), F32))
    d_rot = unstack_heads(total.astype(B16), heads).astype(F32)
    cos_lanes, sin_lanes = cos_ref[...], sin_ref[...]
    d_lin = [rotate_lanes(d_rot[:, i:i + 128], cos_lanes, -sin_lanes, head_dim) for i in range(0, heads * head_dim, 128)]
    dq_ref[...] = jnp.concatenate(d_lin, axis=1).T.astype(B16)

    @pl.when(step == pl.num_programs(0) - 1)
    def _():
        dk_ref[...] = dk_acc[...].astype(B16)
        dv_ref[...] = dv_acc[...].astype(B16)


def attention_backward(q_rot, d_attn, k_rot, v_lin, row_max, inv_sum, cos_lanes, sin_lanes, heads):
    seq_len, width = q_rot.shape
    head_dim = width // heads
    rows = heads * BLOCK
    steps = seq_len // BLOCK
    whole = pl.BlockSpec((seq_len, head_dim), lambda i: (0, 0))
    whole_t = pl.BlockSpec((head_dim, seq_len), lambda i: (0, 0))
    tokens = pl.BlockSpec((BLOCK, width), lambda i: (i, 0))
    stats = pl.BlockSpec((rows, 1), lambda i: (i, 0))
    grad_t = jax.ShapeDtypeStruct((head_dim, seq_len), B16)
    table = pl.BlockSpec((BLOCK, 128), lambda i: (i, 0))
    return pl.pallas_call(
        functools.partial(attention_backward_kernel, heads, head_dim, head_dim ** -0.5),
        grid=(steps,),
        out_shape=(jax.ShapeDtypeStruct((width, seq_len), B16), grad_t, grad_t),
        in_specs=[tokens, tokens, whole, whole, stats, stats, table, table],
        out_specs=(pl.BlockSpec((width, BLOCK), lambda i: (0, i)), whole_t, whole_t),
        scratch_shapes=[
            pltpu.VMEM((rows, seq_len), F32),
            pltpu.VMEM((rows, seq_len), B16),
            pltpu.VMEM((rows, 128), F32),
            pltpu.VMEM((head_dim, seq_len), F32),
            pltpu.VMEM((head_dim, seq_len), F32),
        ],
        compiler_params=pltpu.CompilerParams(vmem_limit_bytes=48 * 1024 * 1024),
        cost_estimate=pl.CostEstimate(flops=40_000_000_000, bytes_accessed=6_000_000, transcendentals=8_000_000),
        name='attention_backward',
    )(q_rot, d_attn, k_rot, v_lin, row_max, inv_sum, cos_lanes, sin_lanes)


def swap_halves(values, head_dim):
    half = head_dim // 2
    lanes = values.shape[1]
    lane = lax.broadcasted_iota(jnp.int32, values.shape, 1)
    return jnp.where(lane % head_dim < half, pltpu.roll(values, lanes - half, 1), pltpu.roll(values, half, 1))


def rotate_lanes(values, cos_lanes, sin_lanes, head_dim):
    return values * cos_lanes + swap_halves(values, head_dim) * sin_lanes


def qkv_kernel(head_dim, me_ref, x_ref, gain_ref, w_ref, cos_ref, sin_ref, q_ref, k_ref, v_ref, u_rows_ref, x_rows_ref):
    width = q_ref.shape[1]
    hidden = x_ref[...].astype(F32)
    inv_rms = inverse_rms(hidden)
    normed = (hidden * inv_rms * gain_ref[...]).astype(B16)
    own = pl.ds(pl.multiple_of(me_ref[0] * u_rows_ref.shape[1], 128), u_rows_ref.shape[1])
    scaled = x_ref[:, own].astype(F32) * inv_rms
    x_rows_ref[...] = scaled
    u_rows_ref[...] = (scaled * gain_ref[:, own]).astype(B16)
    lin = jnp.dot(normed, w_ref[...], preferred_element_type=F32).astype(B16)
    cos_lanes, sin_lanes = cos_ref[...], sin_ref[...]
    rotated = [rotate_lanes(lin[:, i:i + 128].astype(F32), cos_lanes, sin_lanes, head_dim).astype(B16) for i in range(0, width + 128, 128)]
    q_ref[...] = jnp.concatenate(rotated[:-1], axis=1)
    k_ref[...] = rotated[-1][:, :head_dim]
    v_ref[...] = lin[:, width + head_dim:]


def project_qkv(me, x_full, gain, w_qkv, cos_lanes, sin_lanes, head_dim):
    seq_len, model_dim = x_full.shape
    width = w_qkv.shape[1] - 2 * head_dim
    part = BLOCK

    def tile(cols):
        return pl.BlockSpec((BLOCK, cols), lambda i, me_ref: (i, 0))

    def whole(shape):
        return pl.BlockSpec(shape, lambda i, me_ref: (0, 0))

    return pl.pallas_call(
        functools.partial(qkv_kernel, head_dim),
        grid_spec=pltpu.PrefetchScalarGridSpec(
            num_scalar_prefetch=1,
            grid=(seq_len // BLOCK,),
            in_specs=[tile(model_dim), whole((1, model_dim)), whole(w_qkv.shape), tile(128), tile(128)],
            out_specs=(tile(width), tile(head_dim), tile(head_dim), tile(part), tile(part)),
        ),
        out_shape=(
            jax.ShapeDtypeStruct((seq_len, width), B16),
            jax.ShapeDtypeStruct((seq_len, head_dim), B16),
            jax.ShapeDtypeStruct((seq_len, head_dim), B16),
            jax.ShapeDtypeStruct((seq_len, part), B16),
            jax.ShapeDtypeStruct((seq_len, part), F32),
        ),
        compiler_params=pltpu.CompilerParams(vmem_limit_bytes=32 * 1024 * 1024),
        cost_estimate=pl.CostEstimate(flops=3_000_000_000, bytes_accessed=14_000_000, transcendentals=0),
        name='project_qkv',
    )(me.reshape(1), x_full, gain, w_qkv, cos_lanes, sin_lanes)


def hold_weights(me_ref, held_refs, block_refs):
    count = held_refs[0].shape[0]

    @pl.when(pl.program_id(0) == 0)
    def _():
        for i, held in enumerate(held_refs):
            for k, ref in zip((0,) + XOR_ORDER, block_refs[i * count:(i + 1) * count]):
                held[lax.bitwise_xor(me_ref[0], k)] = ref[0]

    return [held[...].reshape(count * held.shape[1], held.shape[2]) for held in held_refs]


def mlp_forward_kernel(me_ref, h_ref, gain_ref, down_ref, *refs):
    weight_refs, out_refs, held_refs = refs[:-8], refs[-8:-2], refs[-2:]
    m_ref, gate_ref, up_ref, glu_ref, y_left_ref, y_right_ref = out_refs
    w_gate, w_up = hold_weights(me_ref, held_refs, weight_refs)
    hidden = h_ref[...].astype(F32)
    mlp_in = (hidden * inverse_rms(hidden) * gain_ref[...]).astype(B16)
    m_ref[...] = mlp_in
    gate_ref[...] = gate = jnp.dot(mlp_in, w_gate, preferred_element_type=F32).astype(B16)
    up_ref[...] = up = jnp.dot(mlp_in, w_up, preferred_element_type=F32).astype(B16)
    glu_ref[...] = glu = gated_unit(gate.astype(F32), up.astype(F32)).astype(B16)
    half = y_left_ref.shape[1]
    y_left_ref[...] = jnp.dot(glu, down_ref[:, :half], preferred_element_type=F32)
    y_right_ref[...] = jnp.dot(glu, down_ref[:, half:], preferred_element_type=F32)


def mlp_backward_kernel(me_ref, gate_ref, up_ref, dy_ref, down_ref, *refs):
    weight_refs, (da_ref, db_ref, dm_ref), held_refs = refs[:-5], refs[-5:-2], refs[-2:]
    w_gate, w_up = hold_weights(me_ref, held_refs, weight_refs)
    gate, up = gate_ref[...].astype(F32), up_ref[...].astype(F32)
    d_glu = dot_f32(dy_ref[...], down_ref[...], ((1,), (1,))).astype(B16).astype(F32)
    sig = jax.nn.sigmoid(gate)
    silu = gate * sig
    da_ref[...] = d_gate = (d_glu * up * (sig + silu * (1.0 - sig))).astype(B16)
    db_ref[...] = d_up = (d_glu * silu).astype(B16)
    dm_ref[...] = dot_f32(d_gate, w_gate, ((1,), (1,))) + dot_f32(d_up, w_up, ((1,), (1,)))


def token_tile(cols):
    return pl.BlockSpec((BLOCK, cols), lambda i, me_ref: (i, 0))


def whole_block(shape):
    return pl.BlockSpec(shape, lambda i, me_ref: (0,) * len(shape))


def mlp_call(kernel, me, operands, operand_specs, weights, out_cols, out_types, flops):
    seq_len = operands[0].shape[0]
    count, rows, part = weights[0].shape
    own_spec = pl.BlockSpec((1, rows, part), lambda i, me_ref: (me_ref[0], 0, 0))
    came_spec = whole_block((1, rows, part))
    weight_specs = ([own_spec] + [came_spec] * (count - 1)) * 2
    return pl.pallas_call(
        kernel,
        grid_spec=pltpu.PrefetchScalarGridSpec(
            num_scalar_prefetch=1,
            grid=(seq_len // BLOCK,),
            in_specs=operand_specs + weight_specs,
            out_specs=tuple(token_tile(cols) for cols in out_cols),
            scratch_shapes=[pltpu.VMEM((count, rows, part), B16), pltpu.VMEM((count, rows, part), B16)],
        ),
        out_shape=tuple(jax.ShapeDtypeStruct((seq_len, cols), dtype) for cols, dtype in zip(out_cols, out_types)),
        compiler_params=pltpu.CompilerParams(vmem_limit_bytes=60 * 1024 * 1024),
        cost_estimate=pl.CostEstimate(flops=flops, bytes_accessed=40_000_000, transcendentals=2_000_000),
    )(me.reshape(1), *operands, *weights)


def ffn_grad_kernel(me_ref, m_ref, da_ref, db_ref, gate_ref, up_ref, da_t, db_t):
    @pl.when(pl.program_id(0) == 0)
    def _():
        da_t[...] = da_ref[...].T
        db_t[...] = db_ref[...].T

    gate_ref[0] = jnp.dot(da_t[...], m_ref[...], preferred_element_type=F32)
    up_ref[0] = jnp.dot(db_t[...], m_ref[...], preferred_element_type=F32)


def ffn_grads(me, mlp_in, d_gate_act, d_up_act, count):
    seq_len, model_dim = mlp_in.shape
    rows, part = model_dim // count, d_gate_act.shape[1]
    block = pl.BlockSpec((1, part, rows), lambda k, me_ref: (k, 0, 0))
    shape = jax.ShapeDtypeStruct((count, part, rows), F32)
    return pl.pallas_call(
        ffn_grad_kernel,
        grid_spec=pltpu.PrefetchScalarGridSpec(
            num_scalar_prefetch=1,
            grid=(count,),
            in_specs=[pl.BlockSpec((seq_len, rows), lambda k, me_ref: (0, lax.bitwise_xor(me_ref[0], k)))] + [whole_block((seq_len, part))] * 2,
            out_specs=(block, block),
            scratch_shapes=[pltpu.VMEM((part, seq_len), B16), pltpu.VMEM((part, seq_len), B16)],
        ),
        out_shape=(shape, shape),
        compiler_params=pltpu.CompilerParams(vmem_limit_bytes=40 * 1024 * 1024),
        cost_estimate=pl.CostEstimate(flops=12_000_000_000, bytes_accessed=26_000_000, transcendentals=0),
        name='ffn_grads',
    )(me.reshape(1), mlp_in, d_gate_act, d_up_act)


def join_kernel(me_ref, *refs):
    blocks, out_ref, held = refs[:-2], refs[-2], refs[-1]
    for k, ref in zip((0,) + XOR_ORDER, blocks):
        held[lax.bitwise_xor(me_ref[0], k)] = ref[0]
    count, width, rows = held.shape
    for pair in range(count // 2):
        out_ref[:, pair * 2 * width:(pair + 1) * 2 * width] = held[2 * pair:2 * pair + 2].reshape(2 * width, rows).T


def join_columns(me, blocks, came):
    count, width, rows = blocks.shape
    tile = 128
    spec = pl.BlockSpec((1, width, tile), lambda i, me_ref: (0, 0, i))
    return pl.pallas_call(
        join_kernel,
        grid_spec=pltpu.PrefetchScalarGridSpec(
            num_scalar_prefetch=1,
            grid=(rows // tile,),
            in_specs=[spec] * count,
            out_specs=pl.BlockSpec((tile, count * width), lambda i, me_ref: (i, 0)),
            scratch_shapes=[pltpu.VMEM((count, width, tile), blocks.dtype)],
        ),
        out_shape=jax.ShapeDtypeStruct((rows, count * width), blocks.dtype),
        compiler_params=pltpu.CompilerParams(vmem_limit_bytes=32 * 1024 * 1024),
        cost_estimate=pl.CostEstimate(flops=1_000_000, bytes_accessed=12_000_000, transcendentals=0),
        name='join_columns',
    )(me.reshape(1), blocks, *came)


def pair_heads_kernel(k_ref, v_ref, out_ref):
    width = k_ref.shape[1] // 4
    parts = [ref[:, h * width:(h + 1) * width] for h in range(4) for ref in (k_ref, v_ref)]
    out_ref[...] = jnp.concatenate(parts, axis=1)


def pair_heads(wk_rows, wv_rows):
    rows, cols = wk_rows.shape
    return pl.pallas_call(pair_heads_kernel, out_shape=jax.ShapeDtypeStruct((rows, 2 * cols), B16), name='pair_heads')(wk_rows, wv_rows)


def qkv_grad_kernel(width, head_dim, g_ref, u_ref, x_ref, wq_ref, wkv_ref, cos_ref, sin_ref, dwq_ref, dwkv_ref, du_ref, dg_ref, acc_ref, share_ref):
    step = pl.program_id(0)
    half = head_dim // 2

    @pl.when(step == 0)
    def _():
        acc_ref[...] = jnp.zeros_like(acc_ref)

    dq = g_ref[0, :width, :]
    dwq_ref[...] = jnp.dot(dq, u_ref[...], preferred_element_type=F32).T
    acc_ref[...] += jnp.dot(wq_ref[...], dq, preferred_element_type=F32)
    share = g_ref[0, width:width + 2 * head_dim, :].astype(F32)

    @pl.when(step % 2 == 0)
    def _():
        share_ref[...] = share

    @pl.when(step % 2 == 1)
    def _():
        summed = (share_ref[...] + share).astype(B16)
        first, second = summed[:half].astype(F32), summed[half:head_dim].astype(F32)
        cos_rows, sin_rows = cos_ref[...], sin_ref[...]
        dk = jnp.concatenate([first * cos_rows + second * sin_rows, second * cos_rows - first * sin_rows], axis=0).astype(B16)
        dkv = jnp.concatenate([dk, summed[head_dim:]], axis=0)
        dwkv_ref[...] = jnp.dot(dkv, u_ref[...], preferred_element_type=F32).T
        acc_ref[...] += jnp.dot(wkv_ref[...], dkv, preferred_element_type=F32)

    @pl.when(step == pl.num_programs(0) - 1)
    def _():
        d_normed = acc_ref[...].T.astype(B16)
        du_ref[...] = d_normed
        dg_ref[...] = jnp.sum(d_normed.astype(F32) * x_ref[...], axis=0, keepdims=True)


def qkv_grads(gathered, u_rows, x_rows, wq_rows, wkv_rows, cos_t, sin_t, head_dim):
    count, height, seq_len = gathered.shape
    rows = u_rows.shape[1]
    width = wq_rows.shape[1] // count

    def whole(shape):
        return pl.BlockSpec(shape, lambda e: (0, 0))

    return pl.pallas_call(
        functools.partial(qkv_grad_kernel, width, head_dim),
        grid=(count,),
        in_specs=[
            pl.BlockSpec((1, height, seq_len), lambda e: (e, 0, 0)),
            whole(u_rows.shape),
            whole(x_rows.shape),
            pl.BlockSpec((rows, width), lambda e: (0, e)),
            pl.BlockSpec((rows, 2 * head_dim), lambda e: (0, e // 2)),
            whole(cos_t.shape),
            whole(sin_t.shape),
        ],
        out_specs=(
            pl.BlockSpec((rows, width), lambda e: (0, e)),
            pl.BlockSpec((rows, 2 * head_dim), lambda e: (0, e // 2)),
            whole((seq_len, rows)),
            whole((1, rows)),
        ),
        out_shape=(
            jax.ShapeDtypeStruct(wq_rows.shape, F32),
            jax.ShapeDtypeStruct(wkv_rows.shape, F32),
            jax.ShapeDtypeStruct((seq_len, rows), B16),
            jax.ShapeDtypeStruct((1, rows), F32),
        ),
        scratch_shapes=[pltpu.VMEM((rows, seq_len), F32), pltpu.VMEM((2 * head_dim, seq_len), F32)],
        compiler_params=pltpu.CompilerParams(vmem_limit_bytes=40 * 1024 * 1024),
        cost_estimate=pl.CostEstimate(flops=5_000_000_000, bytes_accessed=24_000_000, transcendentals=0),
        name='qkv_grads',
    )(gathered, u_rows, x_rows, wq_rows, wkv_rows, cos_t, sin_t)


def solution(mesh):
    n_dev = mesh.shape['sp']
    gather_rows = functools.partial(lax.all_gather, axis_name='sp', axis=0, tiled=True)
    scatter_rows = functools.partial(lax.psum_scatter, axis_name='sp', scatter_dimension=0, tiled=True)
    swap_blocks = functools.partial(lax.all_to_all, axis_name='sp', split_axis=0, concat_axis=0, tiled=True)

    def send_blocks(others):
        others = lax.optimization_barrier(tuple(with_layout_constraint(other, Layout((0, 1, 2))) for other in others))
        came = []
        for k, other in zip(XOR_ORDER, others):
            came.append(with_layout_constraint(lax.ppermute(other, 'sp', [(i, i ^ k) for i in range(n_dev)]), Layout((0, 1, 2))))
        return came

    def pick_blocks(blocks):
        me = lax.axis_index('sp')
        return [lax.dynamic_index_in_dim(blocks, lax.bitwise_xor(me, k), axis=0, keepdims=True) for k in XOR_ORDER]

    def after(value, *others):
        return lax.optimization_barrier((value,) + others)[0]

    def to_tokens(columns):
        blocks = swap_blocks(columns.reshape(n_dev, -1, columns.shape[1]))
        return blocks.transpose(1, 0, 2).reshape(blocks.shape[1], -1)

    def layer_step(x_in, positions, d_out, norm1_gain, norm2_gain, w_q, w_k, w_v, w_o, w_gate, w_up, w_down):
        tokens, model_dim = x_in.shape
        rows = model_dim // n_dev
        seq_len = tokens * n_dev
        q_heads, head_dim = w_q.shape[1:]
        kv_heads = w_k.shape[1]
        heads = q_heads // n_dev
        width = heads * head_dim
        kv_repeat = n_dev // kv_heads
        ffn_part = w_down.shape[0]
        me = lax.axis_index('sp')
        own_rows = functools.partial(lax.dynamic_slice_in_dim, start_index=me * rows, slice_size=rows, axis=1)

        x_full = gather_rows(x_in)
        wq_rows = w_q.reshape(rows, q_heads * head_dim)
        wk_rows = w_k.reshape(rows, kv_heads * head_dim)
        wv_rows = w_v.reshape(rows, kv_heads * head_dim)
        wo_rows = w_o.reshape(width, model_dim)

        wq_blocks = wq_rows.reshape(rows, n_dev, width).transpose(1, 0, 2)
        wk_blocks = jnp.repeat(w_k.transpose(1, 0, 2), kv_repeat, axis=0)
        wv_blocks = jnp.repeat(w_v.transpose(1, 0, 2), kv_repeat, axis=0)
        qkv_blocks = jnp.concatenate([wq_blocks, wk_blocks, wv_blocks], axis=2)
        lane_width = qkv_blocks.shape[2]
        small = jnp.stack([norm1_gain, norm2_gain, (positions // 128).astype(B16), (positions % 128).astype(B16)])
        small = jnp.pad(small, ((0, 12), (0, lane_width - rows)))
        small = jnp.broadcast_to(small[None], (n_dev,) + small.shape)
        qkv_cols = swap_blocks(jnp.concatenate([qkv_blocks, small], axis=1))
        w_qkv = qkv_cols[:, :rows].reshape(model_dim, lane_width)
        gain1 = qkv_cols[:, rows, :rows].reshape(model_dim).astype(F32)
        gain2 = qkv_cols[:, rows + 1, :rows].reshape(model_dim).astype(F32)
        pos_all = (qkv_cols[:, rows + 2, :rows].astype(F32) * 128.0 + qkv_cols[:, rows + 3, :rows].astype(F32)).reshape(seq_len)

        wo_full = gather_rows(wo_rows)
        dy_full = gather_rows(d_out)
        gate_blocks = w_gate.reshape(rows, n_dev, ffn_part).transpose(1, 0, 2)
        up_blocks = w_up.reshape(rows, n_dev, ffn_part).transpose(1, 0, 2)
        gate_others, up_others = pick_blocks(gate_blocks), pick_blocks(up_blocks)
        gate_others, up_others, x_full = lax.optimization_barrier((gate_others, up_others, x_full))
        gate_came, up_came = send_blocks(gate_others), send_blocks(up_others)

        cos_tab, sin_tab = rope_tables(pos_all, head_dim)
        cos_tab, sin_tab = cos_tab[:, 0], sin_tab[:, 0]
        cos_lanes = jnp.tile(cos_tab, (1, 4))
        sin_lanes = jnp.tile(jnp.concatenate([-sin_tab, sin_tab], axis=1), (1, 2))
        q_rot, k_rot, v_lin, u_rows, x_rows = project_qkv(me, x_full, gain1[None], w_qkv, cos_lanes, sin_lanes, head_dim)
        attn_cols, row_max, inv_sum = attention_forward(q_rot, k_rot, v_lin, heads)
        attn_tok = to_tokens(attn_cols)
        hidden = (x_in.astype(F32) + jnp.dot(attn_tok, wo_full, preferred_element_type=F32)).astype(B16)
        h_full = gather_rows(hidden)
        wk_late, wv_late = lax.optimization_barrier((wk_rows, wv_rows, hidden))[:2]
        wkv_rows = pair_heads(wk_late, wv_late)
        weights = (gate_blocks, *gate_came, up_blocks, *up_came)
        half = model_dim // 2
        mlp_in, gate_act, up_act, glu_out, y_left, y_right = mlp_call(
            mlp_forward_kernel, me, (h_full, gain2[None], w_down),
            [token_tile(model_dim), whole_block((1, model_dim)), whole_block(w_down.shape)],
            weights, (model_dim, ffn_part, ffn_part, ffn_part, half, half), (B16, B16, B16, B16, F32, F32), 18_000_000_000)
        y_left = scatter_rows(y_left)
        d_gate_act, d_up_act, d_mlp_part = mlp_call(
            mlp_backward_kernel, me, (gate_act, up_act, dy_full, w_down),
            [token_tile(ffn_part), token_tile(ffn_part), token_tile(model_dim), whole_block(w_down.shape)],
            weights, (ffn_part, ffn_part, model_dim), (B16, B16, F32), 18_000_000_000)
        d_mlp_sum = scatter_rows(d_mlp_part)
        d_gate_blocks, d_up_blocks = ffn_grads(me, mlp_in, d_gate_act, d_up_act, n_dev)
        d_gate_came = send_blocks([d_gate_blocks[k:k + 1] for k in XOR_ORDER])
        d_down = jnp.einsum('tf,td->fd', glu_out, dy_full, preferred_element_type=F32)
        d_mlp_sum, y_right, d_down, d_up_blocks = lax.optimization_barrier((d_mlp_sum, y_right, d_down, d_up_blocks))
        d_mlp_in = d_mlp_sum.astype(B16).astype(F32)
        hidden_f = hidden.astype(F32)
        inv2 = inverse_rms(hidden_f)
        d_hidden = (d_out.astype(F32) + norm_backward(d_mlp_in, hidden_f, inv2, gain2)).astype(B16)
        d_g2_part = jnp.sum(d_mlp_in * hidden_f * inv2, axis=0)
        dh_full = gather_rows(d_hidden)
        d_gate = join_columns(me, d_gate_blocks, d_gate_came)
        d_up_blocks = after(d_up_blocks, dh_full)
        d_up = join_columns(me, d_up_blocks, send_blocks([d_up_blocks[k:k + 1] for k in XOR_ORDER]))

        d_attn = jnp.einsum('td,cd->tc', dh_full, wo_rows, preferred_element_type=F32).astype(B16)
        dq_t, dk_t, dv_t = attention_backward(q_rot, d_attn, k_rot, v_lin, row_max, inv_sum, cos_lanes, sin_lanes, heads)
        d_wo = jnp.einsum('tc,td->cd', attn_cols, dh_full, preferred_element_type=F32)
        piece_hi = lax.reduce_precision(d_g2_part, 8, 7)
        piece_mid = lax.reduce_precision(d_g2_part - piece_hi, 8, 7)
        piece_lo = lax.reduce_precision(d_g2_part - piece_hi - piece_mid, 8, 7)
        pieces = jnp.pad(jnp.stack([piece_hi, piece_mid, piece_lo]).astype(B16), ((0, 13), (0, 0)))
        dqkv_t = gather_rows(jnp.concatenate([dq_t, dk_t, dv_t, pieces], axis=0)).reshape(n_dev, width + 2 * head_dim + 16, seq_len)
        d_g2 = jnp.sum(own_rows(dqkv_t[:, width + 2 * head_dim:width + 2 * head_dim + 3].reshape(-1, seq_len)).astype(F32), axis=0)
        dqkv_t, y_right, d_wo, d_gate, d_up = lax.optimization_barrier((dqkv_t, y_right, d_wo, d_gate, d_up))
        y_right = scatter_rows(y_right)
        y_out = (hidden_f + jnp.concatenate([y_left, y_right], axis=1)).astype(B16)

        d_wq, d_wkv, d_norm_cols, d_g1 = qkv_grads(dqkv_t, u_rows, x_rows, wq_rows, wkv_rows, cos_tab.T, sin_tab.T, head_dim)
        d_wkv = d_wkv.reshape(rows, kv_heads, 2, head_dim)
        d_wk, d_wv = d_wkv[:, :, 0], d_wkv[:, :, 1]
        d_g1 = d_g1[0]
        d_normed = to_tokens(d_norm_cols).astype(F32)
        x_f32 = x_in.astype(F32)
        d_x = (d_hidden.astype(F32) + norm_backward(d_normed, x_f32, inverse_rms(x_f32), gain1)).astype(B16)
        return (y_out, d_x, d_g1, d_g2, d_wq.reshape(w_q.shape), d_wk.reshape(w_k.shape), d_wv.reshape(w_v.shape), d_wo.reshape(w_o.shape), d_gate, d_up, d_down)

    all_rows = P('sp')
    return jax.shard_map(layer_step, mesh=mesh, in_specs=(all_rows,) * 12, out_specs=(all_rows,) * 11, check_vma=False)
```

time: 1790 us -> 898 us (0.50)
  waiting for transfers between devices: 1170 us -> 518 us
  matrix products: 348 us -> 27.4 us
  Pallas kernels: 0 us -> 200 us
  blocking collectives: 118 us -> 0 us
  other arithmetic: 81.1 us -> 18.6 us
  local copies, waits for them, and re-layouts: 38.9 us -> 79.1 us
  starting transfers between devices: 9.9 us -> 30.9 us
    reduce_scatter x7 -> x3, waiting for transfers between devices: 859 us -> 135 us  [the longest x1 72.9 us: layer_step(): d_mlp_sum = scatter_rows(d_mlp_part)]
    dot_general x21 -> x4, matrix products: 327 us -> 27.4 us  [the longest x1 10.5 us: layer_step(): jnp.einsum('tf,td->fd', glu_out, dy_full, preferred_element_type=F32)]
    ppermute x0 -> x28, waiting for transfers between devices: none -> 244 us  [send_blocks(): lax.ppermute(other, 'sp', [(i, i ^ k) for i in range(n_dev)])]
    pallas_call x0 -> x10, Pallas kernels: none -> 200 us  [the longest x2 63.4 us: mlp_call(): pl.pallas_call(kernel, grid_spec=pltpu.PrefetchScalarGridSpec(num_scalar_...]
    all_gather x7 -> x6, waiting for transfers between devices: 282 us -> 95 us  [the longest x1 48.7 us: layer_step(): dh_full = gather_rows(d_hidden)]
    all_to_all x4 -> x0, blocking collectives: 50.9 us -> none  [the longest x1 17.1 us: layer_step(): d_q_rot = to_tokens(d_q_seq.reshape(seq_len, -1, head_dim))]
    another operation x5 -> x3, other arithmetic: 46.1 us -> 0.08 us  [the longest x1 0.04 us: layer_step(): jnp.stack([piece_hi, piece_mid, piece_lo]).astype(B16)]
    all_gather x2 -> x0, blocking collectives: 44.7 us -> none  [layer_step(): gather_rows(shard_w)]
  transfers between devices with their start and end apart: 18 -> 40, of which waited for: 12 -> 29; matrix products, arithmetic and copies ran while one was open for 17% -> 9% of each run, Pallas kernels for 0% -> 13%
where the time goes in v1:
time: 898 us; the launch traced here: 888 us
  waiting for transfers between devices  518 us (58%)
  Pallas kernels  200 us (22%)
  local copies, waits for them, and re-layouts  79.1 us (9%)
  starting transfers between devices  30.9 us (3%)
  matrix products  27.4 us (3%)
  other arithmetic  18.6 us (2%)
  between operations  14.8 us (2%)
    ppermute x28, waiting for transfers between devices, send_blocks(): lax.ppermute(other, 'sp', [(i, i ^ k) for i in range(n_dev)])  244 us
    reduce_scatter x1, waiting for transfers between devices, layer_step(): d_mlp_sum = scatter_rows(d_mlp_part)  72.9 us
    pallas_call x2, Pallas kernels, mlp_call(): pl.pallas_call(kernel, grid_spec=pltpu.PrefetchScalarGridSpec(num_scalar_...  63.4 us
    reduce_scatter x1, waiting for transfers between devices, layer_step(): y_right = scatter_rows(y_right)  62.2 us
    all_gather x1, waiting for transfers between devices, layer_step(): dh_full = gather_rows(d_hidden)  48.7 us
    pallas_call x1, Pallas kernels, attention_backward(): pl.pallas_call(functools.partial(attention_backward_kernel, heads, head_d...  48.4 us
    pallas_call x1, Pallas kernels, attention_forward(): pl.pallas_call(functools.partial(attention_forward_kernel, heads, head_di...  37.7 us
    all_to_all x2, waiting for transfers between devices, to_tokens(): blocks = swap_blocks(columns.reshape(n_dev, -1, columns.shape[1]))  37.1 us
  transfers between devices with their start and end apart: 40, of which 29 were waited for; matrix products, arithmetic and copies ran while one was open for 9% of the time, Pallas kernels for 13%

profile of v1, /device:TPU:0, one launch (start us, length us, event | category | flops | bytes accessed | tf_op | source)
XLA Modules:
  0.0 888.3 jit_solution(7563225117483334039)
XLA Ops:
  57.3 22.0 %all-gather.7.cloned.1.call-done.x_ref = bf16[2048,2048]{1,0:T(8,128)(2,1)} async-done(((bf16[256,2048]{1,0:T(8,128)(2,1)}), bf16[2048,2048]{1,0:T(8,128)(2,1)}) %all-gather.7.cloned.1.call-update) | async-done | bytes 8388624 | tf_op jit(solution)/shard_map/all_gather | solution.py:519
  95.1 37.7 %attention_forward.1 = (bf16[2048,256]{1,0:T(8,128)(2,1)S(1)}, f32[8192,1]{1,0:T(8,128)}, f32[8192,1]{1,0:T(8,128)}) custom-call(bf16[2048,256]{1,0:T(8,128)(2,1)S(1)} %get-tuple-element.93.q_ref, bf16[2048,64]{1,0:T(8,128)(2,1)S(1)} %get-tuple-element.94.k_ref, bf16[2048,64]{1,0:T(8,128)(2,1)S(1)} %get-tuple-element.95.v_ref), custom_call_target="tpu_custom_call" | custom-call | flops 20000000000 | bytes 4000000 | tf_op jit(solution)/shard_map/attention_forward/pallas_call | solution.py:114
  137.1 15.3 %all-to-all-done.1 = bf16[8,256,256]{1,2,0:T(8,128)(2,1)} async-done(((bf16[8,256,256]{1,2,0:T(8,128)(2,1)}), bf16[8,256,256]{1,2,0:T(8,128)(2,1)}, u32[]{:S(2)}, u32[]{:S(2)}) %all-to-all-start.1) | async-done | bytes 1048608 | tf_op jit(solution)/shard_map/all_to_all | solution.py:503
  165.1 14.1 %collective-permute-done.7.refs_9_ = bf16[1,256,704]{2,1,0:T(8,128)(2,1)S(1)} collective-permute-done((bf16[1,256,704]{2,1,0:T(8,128)(2,1)}, bf16[1,256,704]{2,1,0:T(8,128)(2,1)S(1)}, u32[]{:S(2)}, u32[]{:S(2)}) %collective-permute-start.7) | collective-permute-done | bytes 360480 | tf_op jit(solution)/shard_map/ppermute | solution.py:492
  216.6 15.9 %collective-permute-done.refs_1_ = bf16[1,256,704]{2,1,0:T(8,128)(2,1)S(1)} collective-permute-done((bf16[1,256,704]{2,1,0:T(8,128)(2,1)}, bf16[1,256,704]{2,1,0:T(8,128)(2,1)S(1)}, u32[]{:S(2)}, u32[]{:S(2)}) %collective-permute-start) | collective-permute-done | bytes 360480 | tf_op jit(solution)/shard_map/ppermute | solution.py:492
  266.9 29.1 %shard_map.203 = (bf16[2048,2048]{1,0:T(8,128)(2,1)}, bf16[2048,704]{1,0:T(8,128)(2,1)}, bf16[2048,704]{1,0:T(8,128)(2,1)}, bf16[2048,704]{1,0:T(8,128)(2,1)}, f...) custom-call(s32[1]{0:T(128)} %bitcast.me_ref, bf16[2048,2048]{1,0:T(8,128)(2,1)} %all-gather.11.cloned.1.call-done.h_ref, ...), custom_call_target="tpu_custom_call" | custom-call | flops 17999998976 | bytes 40000000 | tf_op jit(solution)/shard_map/pallas_call | solution.py:323
  296.0 20.2 %all-gather.13.cloned.1.call-done.dy_ref = bf16[2048,2048]{1,0:T(8,128)(2,1)} async-done(((bf16[256,2048]{1,0:T(8,128)(2,1)}), bf16[2048,2048]{1,0:T(8,128)(2,1)}) %all-gather.13.cloned.1.call-update) | async-done | bytes 8388624 | tf_op jit(solution)/shard_map/all_gather | solution.py:540
  316.2 34.3 %shard_map.204 = (bf16[2048,704]{1,0:T(8,128)(2,1)}, bf16[2048,704]{1,0:T(8,128)(2,1)}, f32[2048,2048]{1,0:T(8,128)}) custom-call(s32[1]{0:T(128)} %bitcast.me_ref, bf16[2048,704]{1,0:T(8,128)(2,1)} %get-tuple-element.126.gate_ref, bf16[2048,704]{1,0:T(8,128)(2,1)} %get-tuple-element.127.up_ref, bf16[2048,2048]{1,0:T(8,128)(2,1)} %all-gather.13.cloned.1.call-done.dy_ref, ...), custom_call_target="tpu_custom_call" | custom-call | flops 17999998976 | bytes 40000000 | tf_op jit(solution)/shard_map/pallas_call | solution.py:323
  354.9 17.7 %ffn_grads.1 = (f32[8,704,256]{2,1,0:T(8,128)S(1)}, f32[8,704,256]{2,1,0:T(8,128)}) custom-call(s32[1]{0:T(128)} %bitcast.me_ref, bf16[2048,2048]{1,0:T(8,128)(2,1)} %get-tuple-element.131.m_ref, bf16[2048,704]{1,0:T(8,128)(2,1)S(1)} %copy-done.19, bf16[2048,704]{1,0:T(8,128)(2,1)S(1)} %copy-done.20), custom_call_target="tpu_custom_call" | custom-call | flops 12000000000 | bytes 26000000 | tf_op jit(solution)/shard_map/ffn_grads/pallas_call | solution.py:353
  375.2 10.5 %fusion.31 = f32[704,2048]{1,0:T(8,128)} fusion(bf16[2048,704]{1,0:T(8,128)(2,1)S(1)} %copy-done.61, bf16[2048,2048]{1,0:T(8,128)(2,1)} %all-gather.13.cloned.1.call-done.dy_ref), kind=kOutput, calls=%fused_computation.89 | convolution fusion | flops 5905580032 | bytes 17039360 | tf_op jit(solution)/shard_map/tf,td->fd/dot_general | solution.py:572
  385.6 72.9 %reduce-scatter.6.cloned.1.call-done = f32[256,2048]{1,0:T(8,128)} async-done(((f32[2048,2048]{1,0:T(8,128)}), f32[256,2048]{1,0:T(8,128)}) %reduce-scatter.6.cloned.1.call-update) | async-done | bytes 2097168 | tf_op jit(solution)/shard_map/reduce_scatter | solution.py:569
  462.9 48.7 %all-gather.15.cloned.1.call-done = bf16[2048,2048]{1,0:T(8,128)(2,1)} async-done(((bf16[256,2048]{1,0:T(8,128)(2,1)}), bf16[2048,2048]{1,0:T(8,128)(2,1)}) %all-gather.15.cloned.1.call-update) | async-done | bytes 8388624 | tf_op jit(solution)/shard_map/all_gather | solution.py:579
  517.8 48.4 %attention_backward.1 = (bf16[256,2048]{1,0:T(8,128)(2,1)S(1)}, bf16[64,2048]{1,0:T(8,128)(2,1)S(1)}, bf16[64,2048]{1,0:T(8,128)(2,1)S(1)}) custom-call(bf16[2048,256]{1,0:T(8,128)(2,1)S(1)} %copy-done.16, bf16[2048,256]{1,0:T(8,128)(2,1)S(1)} %convolution_convert_fusion.do_ref, bf16[2048,64]{1,0:T(8,128)(2,1)S(1)} %get-tuple-element.94.k_ref, ...), custom_call_target="tpu_custom_call" | custom-call | flops 40000000000 | bytes 6000000 | tf_op jit(solution)/shard_map/attention_backward/pallas_call | solution.py:191
  577.2 27.8 %collective-permute-done.14.refs_1_ = f32[1,704,256]{2,1,0:T(8,128)S(1)} collective-permute-done((f32[1,704,256]{2,1,0:T(8,128)S(1)}, f32[1,704,256]{2,1,0:T(8,128)S(1)}, u32[]{:S(2)}, u32[]{:S(2)}) %collective-permute-start.14) | collective-permute-done | bytes 720928 | tf_op jit(solution)/shard_map/ppermute | solution.py:492
  611.0 13.1 %collective-permute-done.16.refs_3_ = f32[1,704,256]{2,1,0:T(8,128)S(1)} collective-permute-done((f32[1,704,256]{2,1,0:T(8,128)S(1)}, f32[1,704,256]{2,1,0:T(8,128)S(1)}, u32[]{:S(2)}, u32[]{:S(2)}) %collective-permute-start.16) | collective-permute-done | bytes 720928 | tf_op jit(solution)/shard_map/ppermute | solution.py:492
  625.1 20.7 %collective-permute-done.17.refs_4_ = f32[1,704,256]{2,1,0:T(8,128)S(1)} collective-permute-done((f32[1,704,256]{2,1,0:T(8,128)S(1)}, f32[1,704,256]{2,1,0:T(8,128)S(1)}, u32[]{:S(2)}, u32[]{:S(2)}) %collective-permute-start.17) | collective-permute-done | bytes 720928 | tf_op jit(solution)/shard_map/ppermute | solution.py:492
  647.9 28.8 %collective-permute-done.19.refs_6_ = f32[1,704,256]{2,1,0:T(8,128)S(1)} collective-permute-done((f32[1,704,256]{2,1,0:T(8,128)S(1)}, f32[1,704,256]{2,1,0:T(8,128)S(1)}, u32[]{:S(2)}, u32[]{:S(2)}) %collective-permute-start.19) | collective-permute-done | bytes 720928 | tf_op jit(solution)/shard_map/ppermute | solution.py:492
  683.9 21.1 %collective-permute-done.21.refs_1_ = f32[1,704,256]{2,1,0:T(8,128)S(1)} collective-permute-done((f32[1,704,256]{2,1,0:T(8,128)S(1)}, f32[1,704,256]{2,1,0:T(8,128)S(1)}, u32[]{:S(2)}, u32[]{:S(2)}) %collective-permute-start.21) | collective-permute-done | bytes 720928 | tf_op jit(solution)/shard_map/ppermute | solution.py:492
  710.3 10.7 %collective-permute-done.23.refs_3_ = f32[1,704,256]{2,1,0:T(8,128)S(1)} collective-permute-done((f32[1,704,256]{2,1,0:T(8,128)S(1)}, f32[1,704,256]{2,1,0:T(8,128)S(1)}, u32[]{:S(2)}, u32[]{:S(2)}) %collective-permute-start.23) | collective-permute-done | bytes 720928 | tf_op jit(solution)/shard_map/ppermute | solution.py:492
  721.1 13.8 %collective-permute-done.24.refs_4_ = f32[1,704,256]{2,1,0:T(8,128)S(1)} collective-permute-done((f32[1,704,256]{2,1,0:T(8,128)S(1)}, f32[1,704,256]{2,1,0:T(8,128)S(1)}, u32[]{:S(2)}, u32[]{:S(2)}) %collective-permute-start.24) | collective-permute-done | bytes 720928 | tf_op jit(solution)/shard_map/ppermute | solution.py:492
  734.8 16.6 %collective-permute-done.25.refs_5_ = f32[1,704,256]{2,1,0:T(8,128)S(1)} collective-permute-done((f32[1,704,256]{2,1,0:T(8,128)S(1)}, f32[1,704,256]{2,1,0:T(8,128)S(1)}, u32[]{:S(2)}, u32[]{:S(2)}) %collective-permute-start.25) | collective-permute-done | bytes 720928 | tf_op jit(solution)/shard_map/ppermute | solution.py:492
  767.2 14.1 %qkv_grads.1 = (f32[256,2048]{1,0:T(8,128)S(1)}, f32[256,512]{1,0:T(8,128)S(1)}, bf16[2048,256]{1,0:T(8,128)(2,1)}, f32[1,256]{1,0:T(1,128)}) custom-call(bf16[8,400,2048]{2,1,0:T(8,128)(2,1)} %bitcast.121, bf16[2048,256]{1,0:T(8,128)(2,1)S(1)} %copy-done.14, f32[2048,256]{1,0:T(8,128)S(1)} %copy-done.12, bf16[256,2048]{1,0:T(8,128)(2,1)S(1)} %copy.155.wq_ref, ...), custom_call_target="tpu_custom_call" | custom-call | flops 5000000000 | bytes 24000000 | tf_op jit(solution)/shard_map/qkv_grads/pallas_call | solution.py:451
  789.9 21.8 %all-to-all-done.2 = bf16[8,256,256]{2,1,0:T(8,128)(2,1)} async-done(((bf16[8,256,256]{2,1,0:T(8,128)(2,1)}), bf16[8,256,256]{2,1,0:T(8,128)(2,1)}, u32[]{:S(2)}, u32[]{:S(2)}) %all-to-all-start.2) | async-done | bytes 1048608 | tf_op jit(solution)/shard_map/all_to_all | solution.py:503
  816.6 62.2 %reduce-scatter.8.cloned.1.call-done = f32[256,1024]{1,0:T(8,128)} async-done(((f32[2048,1024]{1,0:T(8,128)}), f32[256,1024]{1,0:T(8,128)}) %reduce-scatter.8.cloned.1.call-update) | async-done | bytes 1048592 | tf_op jit(solution)/shard_map/reduce_scatter | solution.py:594
  (286 shorter events, 236.1 us)
Async XLA Ops:
  7.2 72.1 %all-gather.7.cloned.1.call-start = ((), (), s32[]{:S(2)}) async-start(), calls=%async_computation.6 | async-start | bytes 9437184 | tf_op jit(solution)/shard_map/all_gather | solution.py:519
  7.9 129.2 %all-gather.9.cloned.1.call-start = ((), (), s32[]{:S(2)}) async-start(), calls=%async_computation.7 | async-start | bytes 9437184 | tf_op jit(solution)/shard_map/all_gather | solution.py:539
  137.0 129.9 %all-gather.11.cloned.1.call-start = ((), (), s32[]{:S(2)}) async-start(), calls=%async_computation.8 | async-start | bytes 9437184 | tf_op jit(solution)/shard_map/all_gather | solution.py:555
  159.6 156.6 %all-gather.13.cloned.1.call-start = ((), (), s32[]{:S(2)}) async-start(), calls=%async_computation.10 | async-start | bytes 9437184 | tf_op jit(solution)/shard_map/all_gather | solution.py:540
  160.2 298.3 %reduce-scatter.6.cloned.1.call-start = ((), (), s32[]{:S(2)}) async-start(), calls=%async_computation.11 | async-start | bytes 18874368 | tf_op jit(solution)/shard_map/reduce_scatter | solution.py:569
  164.2 41.5 %collective-permute-start.11 = (bf16[1,256,704]{2,1,0:T(8,128)(2,1)}, bf16[1,256,704]{2,1,0:T(8,128)(2,1)S(1)}, u32[]{:S(2)}, u32[]{:S(2)}) collective-permute-start(bf16[1,256,704]{2,1,0:T(8,128)(2,1)} %bitcast.110), channel_id=1, source_target_pairs={{0,5},{1,4},{2,7},{3,6},{4,1},{5,0},{6,3},{7,2}} | collective-permute-start | bytes 1081352 | tf_op jit(solution)/shard_map/ppermute | solution.py:492
  205.7 42.8 %collective-permute-start.2 = (bf16[1,256,704]{2,1,0:T(8,128)(2,1)}, bf16[1,256,704]{2,1,0:T(8,128)(2,1)}, u32[]{:S(2)}, u32[]{:S(2)}) collective-permute-start(bf16[1,256,704]{2,1,0:T(8,128)(2,1)} %bitcast.105), channel_id=1, source_target_pairs={{0,6},{1,7},{2,4},{3,5},{4,2},{5,3},{6,0},{7,1}} | collective-permute-start | bytes 1081352 | tf_op jit(solution)/shard_map/ppermute | solution.py:492
  213.9 41.4 %collective-permute-start.3 = (bf16[1,256,704]{2,1,0:T(8,128)(2,1)}, bf16[1,256,704]{2,1,0:T(8,128)(2,1)}, u32[]{:S(2)}, u32[]{:S(2)}) collective-permute-start(bf16[1,256,704]{2,1,0:T(8,128)(2,1)} %bitcast.104), channel_id=1, source_target_pairs={{0,3},{1,2},{2,1},{3,0},{4,7},{5,6},{6,5},{7,4}} | collective-permute-start | bytes 1081352 | tf_op jit(solution)/shard_map/ppermute | solution.py:492
  214.8 40.6 %collective-permute-start.4 = (bf16[1,256,704]{2,1,0:T(8,128)(2,1)}, bf16[1,256,704]{2,1,0:T(8,128)(2,1)}, u32[]{:S(2)}, u32[]{:S(2)}) collective-permute-start(bf16[1,256,704]{2,1,0:T(8,128)(2,1)} %bitcast.103), channel_id=1, source_target_pairs={{0,5},{1,4},{2,7},{3,6},{4,1},{5,0},{6,3},{7,2}} | collective-permute-start | bytes 1081352 | tf_op jit(solution)/shard_map/ppermute | solution.py:492
  350.5 161.1 %all-gather.15.cloned.1.call-start = ((), (), s32[]{:S(2)}) async-start(), calls=%async_computation.12 | async-start | bytes 9437184 | tf_op jit(solution)/shard_map/all_gather | solution.py:579
  462.8 292.7 %all-gather.17.cloned.1.call-start = ((), (), s32[]{:S(2)}) async-start(), calls=%async_computation.13 | async-start | bytes 14745600 | tf_op jit(solution)/shard_map/all_gather | solution.py:591
  567.6 249.0 %reduce-scatter.4.cloned.1.call-start = ((), (), s32[]{:S(2)}) async-start(), calls=%async_computation.9 | async-start | bytes 9437184 | tf_op jit(solution)/shard_map/reduce_scatter | solution.py:564
  568.3 310.4 %reduce-scatter.8.cloned.1.call-start = ((), (), s32[]{:S(2)}) async-start(), calls=%async_computation.14 | async-start | bytes 9437184 | tf_op jit(solution)/shard_map/reduce_scatter | solution.py:594
  573.6 50.5 %collective-permute-start.16 = (f32[1,704,256]{2,1,0:T(8,128)S(1)}, f32[1,704,256]{2,1,0:T(8,128)S(1)}, u32[]{:S(2)}, u32[]{:S(2)}) collective-permute-start(f32[1,704,256]{2,1,0:T(8,128)S(1)} %get-tuple-element.145), channel_id=1, source_target_pairs={{0,6},{1,7},{2,4},{3,5},{4,2},{5,3},{6,0},{7,1}} | collective-permute-start | bytes 2162696 | tf_op jit(solution)/shard_map/ppermute | solution.py:492
  575.1 70.7 %collective-permute-start.17 = (f32[1,704,256]{2,1,0:T(8,128)S(1)}, f32[1,704,256]{2,1,0:T(8,128)S(1)}, u32[]{:S(2)}, u32[]{:S(2)}) collective-permute-start(f32[1,704,256]{2,1,0:T(8,128)S(1)} %get-tuple-element.146), channel_id=1, source_target_pairs={{0,3},{1,2},{2,1},{3,0},{4,7},{5,6},{6,5},{7,4}} | collective-permute-start | bytes 2162696 | tf_op jit(solution)/shard_map/ppermute | solution.py:492
  575.5 72.4 %collective-permute-start.18 = (f32[1,704,256]{2,1,0:T(8,128)S(1)}, f32[1,704,256]{2,1,0:T(8,128)S(1)}, u32[]{:S(2)}, u32[]{:S(2)}) collective-permute-start(f32[1,704,256]{2,1,0:T(8,128)S(1)} %get-tuple-element.147), channel_id=1, source_target_pairs={{0,5},{1,4},{2,7},{3,6},{4,1},{5,0},{6,3},{7,2}} | collective-permute-start | bytes 2162696 | tf_op jit(solution)/shard_map/ppermute | solution.py:492
  605.0 71.7 %collective-permute-start.19 = (f32[1,704,256]{2,1,0:T(8,128)S(1)}, f32[1,704,256]{2,1,0:T(8,128)S(1)}, u32[]{:S(2)}, u32[]{:S(2)}) collective-permute-start(f32[1,704,256]{2,1,0:T(8,128)S(1)} %get-tuple-element.148), channel_id=1, source_target_pairs={{0,7},{1,6},{2,5},{3,4},{4,3},{5,2},{6,1},{7,0}} | collective-permute-start | bytes 2162696 | tf_op jit(solution)/shard_map/ppermute | solution.py:492
  611.0 65.7 %collective-permute-start.20 = (f32[1,704,256]{2,1,0:T(8,128)S(1)}, f32[1,704,256]{2,1,0:T(8,128)S(1)}, u32[]{:S(2)}, u32[]{:S(2)}) collective-permute-start(f32[1,704,256]{2,1,0:T(8,128)S(1)} %get-tuple-element.149), channel_id=1, source_target_pairs={{0,1},{1,0},{2,3},{3,2},{4,5},{5,4},{6,7},{7,6}} | collective-permute-start | bytes 2162696 | tf_op jit(solution)/shard_map/ppermute | solution.py:492
  624.1 80.9 %collective-permute-start.21 = (f32[1,704,256]{2,1,0:T(8,128)S(1)}, f32[1,704,256]{2,1,0:T(8,128)S(1)}, u32[]{:S(2)}, u32[]{:S(2)}) collective-permute-start(f32[1,704,256]{2,1,0:T(8,128)S(1)} %get-tuple-element.152), channel_id=1, source_target_pairs={{0,2},{1,3},{2,0},{3,1},{4,6},{5,7},{6,4},{7,5}} | collective-permute-start | bytes 2162696 | tf_op jit(solution)/shard_map/ppermute | solution.py:492
  645.8 59.2 %collective-permute-start.22 = (f32[1,704,256]{2,1,0:T(8,128)S(1)}, f32[1,704,256]{2,1,0:T(8,128)S(1)}, u32[]{:S(2)}, u32[]{:S(2)}) collective-permute-start(f32[1,704,256]{2,1,0:T(8,128)S(1)} %get-tuple-element.153), channel_id=1, source_target_pairs={{0,4},{1,5},{2,6},{3,7},{4,0},{5,1},{6,2},{7,3}} | collective-permute-start | bytes 2162696 | tf_op jit(solution)/shard_map/ppermute | solution.py:492
  681.7 53.1 %collective-permute-start.24 = (f32[1,704,256]{2,1,0:T(8,128)S(1)}, f32[1,704,256]{2,1,0:T(8,128)S(1)}, u32[]{:S(2)}, u32[]{:S(2)}) collective-permute-start(f32[1,704,256]{2,1,0:T(8,128)S(1)} %get-tuple-element.155), channel_id=1, source_target_pairs={{0,3},{1,2},{2,1},{3,0},{4,7},{5,6},{6,5},{7,4}} | collective-permute-start | bytes 2162696 | tf_op jit(solution)/shard_map/ppermute | solution.py:492
  683.0 68.5 %collective-permute-start.25 = (f32[1,704,256]{2,1,0:T(8,128)S(1)}, f32[1,704,256]{2,1,0:T(8,128)S(1)}, u32[]{:S(2)}, u32[]{:S(2)}) collective-permute-start(f32[1,704,256]{2,1,0:T(8,128)S(1)} %get-tuple-element.156), channel_id=1, source_target_pairs={{0,5},{1,4},{2,7},{3,6},{4,1},{5,0},{6,3},{7,2}} | collective-permute-start | bytes 2162696 | tf_op jit(solution)/shard_map/ppermute | solution.py:492
  705.0 46.4 %collective-permute-start.26 = (f32[1,704,256]{2,1,0:T(8,128)S(1)}, f32[1,704,256]{2,1,0:T(8,128)S(1)}, u32[]{:S(2)}, u32[]{:S(2)}) collective-permute-start(f32[1,704,256]{2,1,0:T(8,128)S(1)} %get-tuple-element.157), channel_id=1, source_target_pairs={{0,7},{1,6},{2,5},{3,4},{4,3},{5,2},{6,1},{7,0}} | collective-permute-start | bytes 2162696 | tf_op jit(solution)/shard_map/ppermute | solution.py:492
  705.0 46.4 %collective-permute-start.27 = (f32[1,704,256]{2,1,0:T(8,128)S(1)}, f32[1,704,256]{2,1,0:T(8,128)S(1)}, u32[]{:S(2)}, u32[]{:S(2)}) collective-permute-start(f32[1,704,256]{2,1,0:T(8,128)S(1)} %get-tuple-element.158), channel_id=1, source_target_pairs={{0,1},{1,0},{2,3},{3,2},{4,5},{5,4},{6,7},{7,6}} | collective-permute-start | bytes 2162696 | tf_op jit(solution)/shard_map/ppermute | solution.py:492
  (84 other events, 1982.2 us)
Sparse Core Ops, SparseCore 0:
  9.8 69.3 all-gather.6
  81.1 48.6 all-gather.8
  159.7 107.1 all-gather.10
  268.6 47.5 all-gather.12
  350.6 107.8 reduce-scatter.5
  462.9 48.6 all-gather.14
  567.7 167.2 all-gather.16
  738.4 73.6 reduce-scatter.3
  815.5 63.2 reduce-scatter.7

commit v2 on v1

v2 whole, which is shorter than its diff:
```python
import functools
import jax
import jax.numpy as jnp
from jax import lax
from jax.experimental import pallas as pl
from jax.experimental.pallas import tpu as pltpu
from jax.experimental.layout import Layout, with_layout_constraint
from jax.sharding import PartitionSpec as P

ROPE_BASE = 10000.0
NORM_EPS = 1e-5
NEG_LARGE = -1e30
BLOCK = 256
MLP_BLOCK = 512
MIB = 1024 * 1024
EARLY = 3
NOW = 3
FIRST = 2
XOR_ORDER = (2, 4, 6, 3, 5, 7, 1)
B16 = jnp.bfloat16
F32 = jnp.float32


def inverse_rms(hidden):
    return lax.rsqrt(jnp.mean(hidden * hidden, axis=-1, keepdims=True) + NORM_EPS)


def rope_tables(positions, head_dim):
    half_dim = head_dim // 2
    inv_freq = 1.0 / (ROPE_BASE ** (jnp.arange(half_dim, dtype=F32) * (2.0 / head_dim)))
    angles = positions.astype(F32)[:, None] * inv_freq[None, :]
    return jnp.cos(angles)[:, None, :], jnp.sin(angles)[:, None, :]


def cost(mega_flops):
    return pl.CostEstimate(flops=mega_flops * 1_000_000, bytes_accessed=20_000_000, transcendentals=0)


def gated_unit(gate_pre, up_pre):
    return jax.nn.silu(gate_pre) * up_pre


def norm_backward(d_normed, hidden, inv_rms, gain):
    scaled = d_normed * gain
    row_dot = jnp.mean(scaled * hidden, axis=-1, keepdims=True)
    return inv_rms * scaled - hidden * (inv_rms * inv_rms * inv_rms * row_dot)


def stack_heads(block, heads, head_dim):
    return jnp.concatenate([block[:, h * head_dim:(h + 1) * head_dim] for h in range(heads)], axis=0)


def unstack_heads(rows, heads):
    size = rows.shape[0] // heads
    return jnp.concatenate([rows[h * size:(h + 1) * size] for h in range(heads)], axis=1)


def dot_f32(lhs, rhs, dims):
    return lax.dot_general(lhs, rhs, (dims, ((), ())), preferred_element_type=F32)


def causal_block(heads):
    shape = (heads * BLOCK, BLOCK)
    row = lax.broadcasted_iota(jnp.int32, shape, 0) % BLOCK
    col = lax.broadcasted_iota(jnp.int32, shape, 1)
    return row >= col


def attention_forward_kernel(heads, head_dim, scale, q_ref, k_ref, v_ref, o_ref, max_ref, inv_ref, score_ref, acc_ref):
    step = pl.program_id(0)
    queries = stack_heads(q_ref[:], heads, head_dim)
    last = pl.multiple_of(step * BLOCK, BLOCK)

    def scores_at(start):
        return dot_f32(queries, k_ref[pl.ds(start, BLOCK), :], ((1,), (1,))) * scale

    def fold(op, block):
        return op(block[:, :128], block[:, 128:])

    diag = jnp.where(causal_block(heads), scores_at(last), NEG_LARGE)
    score_ref[:, pl.ds(last, BLOCK)] = diag
    acc_ref[:] = fold(jnp.maximum, diag)

    @pl.loop(0, step)
    def _(j):
        start = pl.multiple_of(j * BLOCK, BLOCK)
        block = scores_at(start)
        score_ref[:, pl.ds(start, BLOCK)] = block
        acc_ref[:] = jnp.maximum(acc_ref[:], fold(jnp.maximum, block))

    row_max = jnp.max(acc_ref[:], axis=1, keepdims=True)
    max_ref[:] = row_max
    acc_ref[:] = jnp.zeros_like(acc_ref)

    @pl.loop(0, step + 1)
    def _(j):
        start = pl.multiple_of(j * BLOCK, BLOCK)
        block = jnp.exp(score_ref[:, pl.ds(start, BLOCK)] - row_max)
        score_ref[:, pl.ds(start, BLOCK)] = block
        acc_ref[:] += fold(jnp.add, block)

    inv_sum = 1.0 / jnp.sum(acc_ref[:], axis=1, keepdims=True)
    inv_ref[:] = inv_sum

    def weighted(j, total):
        start = pl.multiple_of(j * BLOCK, BLOCK)
        probs = (score_ref[:, pl.ds(start, BLOCK)] * inv_sum).astype(B16)
        return total + dot_f32(probs, v_ref[pl.ds(start, BLOCK), :], ((1,), (0,)))

    total = lax.fori_loop(0, step + 1, weighted, jnp.zeros((heads * BLOCK, head_dim), F32))
    o_ref[:] = unstack_heads(total.astype(B16), heads)


def attention_forward(q_rot, k_rot, v_lin, heads):
    seq_len, width = q_rot.shape
    head_dim = width // heads
    rows = heads * BLOCK
    steps = seq_len // BLOCK
    whole = whole_block((seq_len, head_dim))
    tokens = pl.BlockSpec((BLOCK, width), lambda i: (i, 0))
    stats = pl.BlockSpec((rows, 1), lambda i: (i, 0))
    stat_shape = jax.ShapeDtypeStruct((steps * rows, 1), F32)
    return pl.pallas_call(
        functools.partial(attention_forward_kernel, heads, head_dim, head_dim ** -0.5),
        grid=(steps,),
        out_shape=(jax.ShapeDtypeStruct((seq_len, width), B16), stat_shape, stat_shape),
        in_specs=[tokens, whole, whole],
        out_specs=(tokens, stats, stats),
        scratch_shapes=[pltpu.VMEM((rows, seq_len), F32), pltpu.VMEM((rows, 128), F32)],
        compiler_params=pltpu.CompilerParams(vmem_limit_bytes=48 * MIB),
        cost_estimate=cost(20000),
        name='attention_forward',
    )(q_rot, k_rot, v_lin)


def attention_backward_kernel(heads, head_dim, scale, q_ref, do_ref, k_ref, v_ref, max_ref, inv_ref, cos_ref, sin_ref, dq_ref, dk_ref, dv_ref, prob_ref, dp_ref, acc_ref, dk_acc, dv_acc):
    step = pl.program_id(0)
    queries = stack_heads(q_ref[:], heads, head_dim)
    d_out = stack_heads(do_ref[:], heads, head_dim)
    row_max = max_ref[:]
    inv_sum = inv_ref[:]
    last = pl.multiple_of(step * BLOCK, BLOCK)

    @pl.when(step == 0)
    def _():
        dk_acc[:] = jnp.zeros_like(dk_acc)
        dv_acc[:] = jnp.zeros_like(dv_acc)

    def scores_at(start):
        return dot_f32(queries, k_ref[pl.ds(start, BLOCK), :], ((1,), (1,))) * scale

    def first_pass(start, scores):
        probs = jnp.exp(scores - row_max) * inv_sum
        d_probs = dot_f32(d_out, v_ref[pl.ds(start, BLOCK), :], ((1,), (1,))).astype(B16)
        prob_ref[:, pl.ds(start, BLOCK)] = probs
        dp_ref[:, pl.ds(start, BLOCK)] = d_probs
        product = probs * d_probs.astype(F32)
        dv_acc[:, pl.ds(start, BLOCK)] += dot_f32(d_out, probs.astype(B16), ((0,), (0,)))
        return product[:, :128] + product[:, 128:]

    acc_ref[:] = first_pass(last, jnp.where(causal_block(heads), scores_at(last), NEG_LARGE))

    @pl.loop(0, step)
    def _(j):
        start = pl.multiple_of(j * BLOCK, BLOCK)
        acc_ref[:] += first_pass(start, scores_at(start))

    row_dot = jnp.sum(acc_ref[:], axis=1, keepdims=True)

    def second_pass(j, total):
        start = pl.multiple_of(j * BLOCK, BLOCK)
        at = pl.ds(start, BLOCK)
        d_scores = (prob_ref[:, at] * (dp_ref[:, at].astype(F32) - row_dot) * scale).astype(B16)
        dk_acc[:, at] += dot_f32(queries, d_scores, ((0,), (0,)))
        return total + dot_f32(d_scores, k_ref[at, :], ((1,), (0,)))

    total = lax.fori_loop(0, step + 1, second_pass, jnp.zeros((heads * BLOCK, head_dim), F32))
    d_rot = unstack_heads(total.astype(B16), heads).astype(F32)
    cos_lanes, sin_lanes = cos_ref[:], sin_ref[:]
    d_lin = [rotate_lanes(d_rot[:, i:i + 128], cos_lanes, -sin_lanes, head_dim) for i in range(0, heads * head_dim, 128)]
    dq_ref[:] = jnp.concatenate(d_lin, axis=1).T.astype(B16)

    @pl.when(step == pl.num_programs(0) - 1)
    def _():
        dk_ref[:] = dk_acc[:].astype(B16)
        dv_ref[:] = dv_acc[:].astype(B16)


def attention_backward(q_rot, d_attn, k_rot, v_lin, row_max, inv_sum, cos_lanes, sin_lanes, heads):
    seq_len, width = q_rot.shape
    head_dim = width // heads
    rows = heads * BLOCK
    steps = seq_len // BLOCK
    whole = whole_block((seq_len, head_dim))
    whole_t = whole_block((head_dim, seq_len))
    tokens = pl.BlockSpec((BLOCK, width), lambda i: (i, 0))
    stats = pl.BlockSpec((rows, 1), lambda i: (i, 0))
    grad_t = jax.ShapeDtypeStruct((head_dim, seq_len), B16)
    table = pl.BlockSpec((BLOCK, 128), lambda i: (i, 0))
    return pl.pallas_call(
        functools.partial(attention_backward_kernel, heads, head_dim, head_dim ** -0.5),
        grid=(steps,),
        out_shape=(jax.ShapeDtypeStruct((width, seq_len), B16), grad_t, grad_t),
        in_specs=[tokens, tokens, whole, whole, stats, stats, table, table],
        out_specs=(pl.BlockSpec((width, BLOCK), lambda i: (0, i)), whole_t, whole_t),
        scratch_shapes=[
            pltpu.VMEM((rows, seq_len), F32),
            pltpu.VMEM((rows, seq_len), B16),
            pltpu.VMEM((rows, 128), F32),
            pltpu.VMEM((head_dim, seq_len), F32),
            pltpu.VMEM((head_dim, seq_len), F32),
        ],
        compiler_params=pltpu.CompilerParams(vmem_limit_bytes=48 * MIB),
        cost_estimate=cost(40000),
        name='attention_backward',
    )(q_rot, d_attn, k_rot, v_lin, row_max, inv_sum, cos_lanes, sin_lanes)


def peer_of(me, mask):
    result = 0
    for bit in (1, 2, 4):
        mine = lax.rem(me // bit, 2)
        result = result + bit * ((1 - mine) if mask & bit else mine)
    return result


def gather_kernel(split, src_ref, out_ref, send_sem, recv_sem, local_sem):
    me = lax.axis_index('sp')
    rows = src_ref.shape[0]
    across, along, other, diagonal = (peer_of(me, mask) for mask in (2, 4, 1, 6))
    barrier = pltpu.get_barrier_semaphore()
    for device in (across, along, other):
        pl.semaphore_signal(barrier, inc=1, device_id=(device,), device_id_type=pl.DeviceIdType.MESH)
    pl.semaphore_wait(barrier, 3)

    upper, lower = (0, split), (split, rows - split)

    def place(owner, part):
        return out_ref.at[pl.ds(pl.multiple_of(owner * rows + part[0], 16), part[1]), :]

    def own(part):
        return src_ref.at[pl.ds(part[0], part[1]), :]

    plan = [
        (own(upper), place(me, upper), along),
        (own(lower), place(me, lower), across),
        (own(lower), place(me, lower), along),
        (own(upper), place(me, upper), across),
        (own((0, rows)), place(me, (0, rows)), other),
        (place(along, upper), place(along, upper), across),
        (place(across, lower), place(across, lower), along),
        (place(along, upper), place(along, upper), other),
        (place(across, lower), place(across, lower), other),
        (place(along, lower), place(along, lower), other),
        (place(across, upper), place(across, upper), other),
        (place(diagonal, upper), place(diagonal, upper), other),
        (place(diagonal, lower), place(diagonal, lower), other),
    ]
    copies = [
        pltpu.make_async_remote_copy(src_ref=src, dst_ref=dst, send_sem=send_sem.at[i], recv_sem=recv_sem.at[i], device_id=(device,), device_id_type=pl.DeviceIdType.MESH)
        for i, (src, dst, device) in enumerate(plan)
    ]
    for i in range(5):
        copies[i].start()
    mine = pltpu.make_async_copy(src_ref, place(me, (0, rows)), local_sem)
    mine.start()
    for came, go in ((0, (5, 7)), (1, (6, 8)), (2, (9,)), (3, (10,)), (5, (11,)), (6, (12,))):
        copies[came].wait_recv()
        for i in go:
            copies[i].start()
    for i in (4, 7, 8, 9, 10, 11, 12):
        copies[i].wait_recv()
    for copy in copies:
        copy.wait_send()
    mine.wait()


def gather_blocks(block, collective_id):
    rows, cols = block.shape
    split = (rows // 2 + 15) // 16 * 16
    return pl.pallas_call(
        functools.partial(gather_kernel, split),
        out_shape=jax.ShapeDtypeStruct((8 * rows, cols), block.dtype),
        in_specs=[pl.BlockSpec(memory_space=pltpu.VMEM)],
        out_specs=pl.BlockSpec(memory_space=pl.ANY),
        scratch_shapes=[pltpu.SemaphoreType.DMA((13,)), pltpu.SemaphoreType.DMA((13,)), pltpu.SemaphoreType.DMA],
        compiler_params=pltpu.CompilerParams(collective_id=collective_id, has_side_effects=True),
        cost_estimate=cost(30000),
        name='gather_blocks',
    )(block)


def reduce_kernel(part_ref, out_ref, mine, came, first_a, first_b, last_a, last_b, send_sem, recv_sem, local_sem):
    me = lax.axis_index('sp')
    masks = (0, 2, 4, 6)
    across, along, other = (peer_of(me, mask) for mask in (2, 4, 1))
    barrier = pltpu.get_barrier_semaphore()
    for device in (across, along, other):
        pl.semaphore_signal(barrier, inc=1, device_id=(device,), device_id_type=pl.DeviceIdType.MESH)
    pl.semaphore_wait(barrier, 3)
    rows, cols = out_ref.shape
    half = cols // 2
    left, right = pl.ds(0, half), pl.ds(half, half)

    def remote(i, src, dst, device):
        return pltpu.make_async_remote_copy(src_ref=src, dst_ref=dst, send_sem=send_sem.at[i], recv_sem=recv_sem.at[i], device_id=(device,), device_id_type=pl.DeviceIdType.MESH)

    def add(dst, *srcs):
        @pl.loop(0, rows // 32)
        def _(r):
            at = pl.ds(pl.multiple_of(r * 32, 32), 32)
            total = dst[at, :]
            for src in srcs:
                total = total + src[at, :]
            dst[at, :] = total

    order = (3, 1, 2, 0)
    pair = {j: remote(j, part_ref.at[peer_of(me, masks[j] + 1)], came.at[j], other) for j in order}
    local = {j: pltpu.make_async_copy(part_ref.at[peer_of(me, masks[j])], mine.at[j], local_sem.at[j]) for j in order}
    for j in order:
        pair[j].start()
        local[j].start()

    def summed(j):
        local[j].wait()
        pair[j].wait_recv()
        add(mine.at[j], came.at[j])

    far_a = remote(4, mine.at[3, :, left], first_a.at[1], across)
    far_b = remote(5, mine.at[3, :, right], first_b.at[1], along)
    near_a = remote(6, mine.at[1, :, left], first_a.at[0], across)
    near_b = remote(7, mine.at[2, :, right], first_b.at[0], along)
    next_a = remote(8, mine.at[2, :, left], last_a, along)
    next_b = remote(9, mine.at[1, :, right], last_b, across)
    summed(3)
    far_a.start()
    far_b.start()
    summed(1)
    near_a.start()
    summed(2)
    near_b.start()
    summed(0)
    far_a.wait_recv()
    add(mine.at[2, :, left], first_a.at[1])
    next_a.start()
    far_b.wait_recv()
    add(mine.at[1, :, right], first_b.at[1])
    next_b.start()
    near_a.wait_recv()
    add(mine.at[0, :, left], first_a.at[0])
    near_b.wait_recv()
    add(mine.at[0, :, right], first_b.at[0])

    def finish(where, extra):
        @pl.loop(0, rows // 32)
        def _(r):
            at = pl.ds(pl.multiple_of(r * 32, 32), 32)
            out_ref[at, where] = mine[0, at, where] + extra[at, :]

    next_a.wait_recv()
    finish(left, last_a)
    next_b.wait_recv()
    finish(right, last_b)
    for copy in (*pair.values(), far_a, far_b, near_a, near_b, next_a, next_b):
        copy.wait_send()


def reduce_blocks(part, collective_id):
    seq_len, cols = part.shape
    rows = seq_len // 8
    return pl.pallas_call(
        reduce_kernel,
        out_shape=jax.ShapeDtypeStruct((rows, cols), part.dtype),
        in_specs=[pl.BlockSpec(memory_space=pl.ANY)],
        out_specs=pl.BlockSpec(memory_space=pltpu.VMEM),
        scratch_shapes=[
            pltpu.VMEM((4, rows, cols), part.dtype),
            pltpu.VMEM((4, rows, cols), part.dtype),
            pltpu.VMEM((2, rows, cols // 2), part.dtype),
            pltpu.VMEM((2, rows, cols // 2), part.dtype),
            pltpu.VMEM((rows, cols // 2), part.dtype),
            pltpu.VMEM((rows, cols // 2), part.dtype),
            pltpu.SemaphoreType.DMA((10,)),
            pltpu.SemaphoreType.DMA((10,)),
            pltpu.SemaphoreType.DMA((4,)),
        ],
        compiler_params=pltpu.CompilerParams(collective_id=collective_id, has_side_effects=True, vmem_limit_bytes=40 * MIB),
        cost_estimate=cost(60000),
        name='reduce_blocks',
    )(part.reshape(8, rows, cols))


def swap_halves(values, head_dim):
    half = head_dim // 2
    lanes = values.shape[1]
    lane = lax.broadcasted_iota(jnp.int32, values.shape, 1)
    return jnp.where(lane % head_dim < half, pltpu.roll(values, lanes - half, 1), pltpu.roll(values, half, 1))


def rotate_lanes(values, cos_lanes, sin_lanes, head_dim):
    return values * cos_lanes + swap_halves(values, head_dim) * sin_lanes


def qkv_kernel(head_dim, me_ref, x_ref, gain_ref, w_ref, cos_ref, sin_ref, q_ref, k_ref, v_ref, u_rows_ref, x_rows_ref):
    width = q_ref.shape[1]
    hidden = x_ref[:].astype(F32)
    inv_rms = inverse_rms(hidden)
    normed = (hidden * inv_rms * gain_ref[:]).astype(B16)
    own = pl.ds(pl.multiple_of(me_ref[0] * u_rows_ref.shape[1], 128), u_rows_ref.shape[1])
    scaled = x_ref[:, own].astype(F32) * inv_rms
    x_rows_ref[:] = scaled
    u_rows_ref[:] = (scaled * gain_ref[:, own]).astype(B16)
    lin = jnp.dot(normed, w_ref[:], preferred_element_type=F32).astype(B16)
    cos_lanes, sin_lanes = cos_ref[:], sin_ref[:]
    rotated = [rotate_lanes(lin[:, i:i + 128].astype(F32), cos_lanes, sin_lanes, head_dim).astype(B16) for i in range(0, width + 128, 128)]
    q_ref[:] = jnp.concatenate(rotated[:-1], axis=1)
    k_ref[:] = rotated[-1][:, :head_dim]
    v_ref[:] = lin[:, width + head_dim:]


def project_qkv(me, x_full, gain, w_qkv, cos_lanes, sin_lanes, head_dim):
    seq_len, model_dim = x_full.shape
    width = w_qkv.shape[1] - 2 * head_dim
    part = BLOCK

    def tile(cols):
        return pl.BlockSpec((BLOCK, cols), lambda i, me_ref: (i, 0))

    return pl.pallas_call(
        functools.partial(qkv_kernel, head_dim),
        grid_spec=pltpu.PrefetchScalarGridSpec(
            num_scalar_prefetch=1,
            grid=(seq_len // BLOCK,),
            in_specs=[tile(model_dim), whole_block((1, model_dim)), whole_block(w_qkv.shape), tile(128), tile(128)],
            out_specs=(tile(width), tile(head_dim), tile(head_dim), tile(part), tile(part)),
        ),
        out_shape=(
            jax.ShapeDtypeStruct((seq_len, width), B16),
            jax.ShapeDtypeStruct((seq_len, head_dim), B16),
            jax.ShapeDtypeStruct((seq_len, head_dim), B16),
            jax.ShapeDtypeStruct((seq_len, part), B16),
            jax.ShapeDtypeStruct((seq_len, part), F32),
        ),
        compiler_params=pltpu.CompilerParams(vmem_limit_bytes=32 * MIB),
        cost_estimate=cost(3000),
        name='project_qkv',
    )(me.reshape(1), x_full, gain, w_qkv, cos_lanes, sin_lanes)


def hold_weights(me_ref, held_refs, block_refs):
    count = held_refs[0].shape[0]

    @pl.when(pl.program_id(0) == 0)
    def _():
        for i, held in enumerate(held_refs):
            for k, ref in zip((0,) + XOR_ORDER, block_refs[i * count:(i + 1) * count]):
                held[lax.bitwise_xor(me_ref[0], k)] = ref[0]

    return [held[:].reshape(count * held.shape[1], held.shape[2]) for held in held_refs]


def mlp_forward_kernel(me_ref, h_ref, gain_ref, down_ref, *refs):
    weight_refs, out_refs, held_refs = refs[:-7], refs[-7:-2], refs[-2:]
    m_ref, gate_ref, up_ref, glu_ref, y_ref = out_refs
    w_gate, w_up = hold_weights(me_ref, held_refs, weight_refs)
    hidden = h_ref[:].astype(F32)
    mlp_in = (hidden * inverse_rms(hidden) * gain_ref[:]).astype(B16)
    m_ref[:] = mlp_in
    gate_ref[:] = gate = jnp.dot(mlp_in, w_gate, preferred_element_type=F32).astype(B16)
    up_ref[:] = up = jnp.dot(mlp_in, w_up, preferred_element_type=F32).astype(B16)
    glu_ref[:] = glu = gated_unit(gate.astype(F32), up.astype(F32)).astype(B16)
    y_ref[:] = jnp.dot(glu, down_ref[:], preferred_element_type=F32)


def mlp_backward_kernel(me_ref, gate_ref, up_ref, dy_ref, down_ref, *refs):
    weight_refs, (da_ref, db_ref, dm_ref), held_refs = refs[:-5], refs[-5:-2], refs[-2:]
    w_gate, w_up = hold_weights(me_ref, held_refs, weight_refs)
    gate, up = gate_ref[:].astype(F32), up_ref[:].astype(F32)
    d_glu = dot_f32(dy_ref[:], down_ref[:], ((1,), (1,))).astype(B16).astype(F32)
    sig = jax.nn.sigmoid(gate)
    silu = gate * sig
    da_ref[:] = d_gate = (d_glu * up * (sig + silu * (1.0 - sig))).astype(B16)
    db_ref[:] = d_up = (d_glu * silu).astype(B16)
    dm_ref[:] = dot_f32(d_gate, w_gate, ((1,), (1,))) + dot_f32(d_up, w_up, ((1,), (1,)))


def token_tile(cols):
    return pl.BlockSpec((MLP_BLOCK, cols), lambda i, me_ref: (i, 0))


def whole_block(shape):
    return pl.BlockSpec(shape, lambda *ids: (0,) * len(shape))


def mlp_call(kernel, me, operands, operand_specs, weights, out_cols, out_types, flops):
    seq_len = operands[0].shape[0]
    count, rows, part = weights[0].shape
    own_spec = pl.BlockSpec((1, rows, part), lambda i, me_ref: (me_ref[0], 0, 0))
    came_spec = whole_block((1, rows, part))
    weight_specs = ([own_spec] + [came_spec] * (count - 1)) * 2
    return pl.pallas_call(
        kernel,
        grid_spec=pltpu.PrefetchScalarGridSpec(
            num_scalar_prefetch=1,
            grid=(seq_len // MLP_BLOCK,),
            in_specs=operand_specs + weight_specs,
            out_specs=tuple(token_tile(cols) for cols in out_cols),
            scratch_shapes=[pltpu.VMEM((count, rows, part), B16), pltpu.VMEM((count, rows, part), B16)],
        ),
        out_shape=tuple(jax.ShapeDtypeStruct((seq_len, cols), dtype) for cols, dtype in zip(out_cols, out_types)),
        compiler_params=pltpu.CompilerParams(vmem_limit_bytes=60 * MIB),
        cost_estimate=cost(flops),
    )(me.reshape(1), *operands, *weights)


def ffn_grad_kernel(me_ref, m_ref, da_ref, db_ref, *refs):
    out_refs, (da_t, db_t) = refs[:-2], refs[-2:]
    count = len(out_refs) // 2
    step = pl.program_id(0)

    @pl.when(step == 0)
    def _():
        da_t[:] = da_ref[:].T
        db_t[:] = db_ref[:].T

    for k in range(count):
        @pl.when(step == k)
        def _():
            out_refs[k][0] = jnp.dot(da_t[:], m_ref[:], preferred_element_type=F32)
            out_refs[count + k][0] = jnp.dot(db_t[:], m_ref[:], preferred_element_type=F32)


def ffn_grads(me, mlp_in, d_gate_act, d_up_act, count):
    seq_len, model_dim = mlp_in.shape
    rows, part = model_dim // count, d_gate_act.shape[1]
    shape = jax.ShapeDtypeStruct((1, part, rows), F32)
    blocks = pl.pallas_call(
        ffn_grad_kernel,
        grid_spec=pltpu.PrefetchScalarGridSpec(
            num_scalar_prefetch=1,
            grid=(count,),
            in_specs=[pl.BlockSpec((seq_len, rows), lambda k, me_ref: (0, lax.bitwise_xor(me_ref[0], k)))] + [whole_block((seq_len, part))] * 2,
            out_specs=(whole_block(shape.shape),) * (2 * count),
            scratch_shapes=[pltpu.VMEM((part, seq_len), B16), pltpu.VMEM((part, seq_len), B16)],
        ),
        out_shape=(shape,) * (2 * count),
        compiler_params=pltpu.CompilerParams(vmem_limit_bytes=56 * MIB),
        cost_estimate=cost(12000),
        name='ffn_grads',
    )(me.reshape(1), mlp_in, d_gate_act, d_up_act)
    return blocks[:count], blocks[count:]


def join_kernel(me_ref, *refs):
    blocks, out_ref, held = refs[:-2], refs[-2], refs[-1]
    for k, ref in zip((0,) + XOR_ORDER, blocks):
        held[lax.bitwise_xor(me_ref[0], k)] = ref[0]
    count, width, rows = held.shape
    for pair in range(count // 2):
        out_ref[:, pair * 2 * width:(pair + 1) * 2 * width] = held[2 * pair:2 * pair + 2].reshape(2 * width, rows).T


def join_columns(me, own, came):
    count = 1 + len(came)
    width, rows = own.shape[1:]
    tile = 128
    spec = pl.BlockSpec((1, width, tile), lambda i, me_ref: (0, 0, i))
    return pl.pallas_call(
        join_kernel,
        grid_spec=pltpu.PrefetchScalarGridSpec(
            num_scalar_prefetch=1,
            grid=(rows // tile,),
            in_specs=[spec] * count,
            out_specs=pl.BlockSpec((tile, count * width), lambda i, me_ref: (i, 0)),
            scratch_shapes=[pltpu.VMEM((count, width, tile), own.dtype)],
        ),
        out_shape=jax.ShapeDtypeStruct((rows, count * width), own.dtype),
        compiler_params=pltpu.CompilerParams(vmem_limit_bytes=32 * MIB),
        cost_estimate=cost(1),
        name='join_columns',
    )(me.reshape(1), own, *came)


def pair_heads_kernel(k_ref, v_ref, out_ref):
    width = k_ref.shape[1] // 4
    parts = [ref[:, h * width:(h + 1) * width] for h in range(4) for ref in (k_ref, v_ref)]
    out_ref[:] = jnp.concatenate(parts, axis=1)


def pair_heads(wk_rows, wv_rows):
    rows, cols = wk_rows.shape
    return pl.pallas_call(pair_heads_kernel, out_shape=jax.ShapeDtypeStruct((rows, 2 * cols), B16), name='pair_heads')(wk_rows, wv_rows)


def normed_grad_kernel(width, head_dim, g_ref, x_ref, wq_ref, wkv_ref, cos_ref, sin_ref, dkv_ref, du_ref, dg_ref, acc_ref, share_ref):
    step = pl.program_id(0)
    half = head_dim // 2

    @pl.when(step == 0)
    def _():
        acc_ref[:] = jnp.zeros_like(acc_ref)

    acc_ref[:] += jnp.dot(wq_ref[:], g_ref[0, :width, :], preferred_element_type=F32)
    share = g_ref[0, width:width + 2 * head_dim, :].astype(F32)

    @pl.when(step % 2 == 0)
    def _():
        share_ref[:] = share

    @pl.when(step % 2 == 1)
    def _():
        summed = (share_ref[:] + share).astype(B16)
        first, second = summed[:half].astype(F32), summed[half:head_dim].astype(F32)
        cos_rows, sin_rows = cos_ref[:], sin_ref[:]
        dk = jnp.concatenate([first * cos_rows + second * sin_rows, second * cos_rows - first * sin_rows], axis=0).astype(B16)
        dkv = jnp.concatenate([dk, summed[head_dim:]], axis=0)
        dkv_ref[0] = dkv
        acc_ref[:] += jnp.dot(wkv_ref[:], dkv, preferred_element_type=F32)

    @pl.when(step == pl.num_programs(0) - 1)
    def _():
        d_normed = acc_ref[:].T.astype(B16)
        du_ref[:] = d_normed
        dg_ref[:] = jnp.sum(d_normed.astype(F32) * x_ref[:], axis=0, keepdims=True)


def normed_grads(gathered, x_rows, wq_rows, wkv_rows, cos_t, sin_t, head_dim):
    count, height, seq_len = gathered.shape
    rows = x_rows.shape[1]
    width = wq_rows.shape[1] // count

    return pl.pallas_call(
        functools.partial(normed_grad_kernel, width, head_dim),
        grid=(count,),
        in_specs=[
            pl.BlockSpec((1, height, seq_len), lambda e: (e, 0, 0)),
            whole_block(x_rows.shape),
            pl.BlockSpec((rows, width), lambda e: (0, e)),
            pl.BlockSpec((rows, 2 * head_dim), lambda e: (0, e // 2)),
            whole_block(cos_t.shape),
            whole_block(sin_t.shape),
        ],
        out_specs=(pl.BlockSpec((1, 2 * head_dim, seq_len), lambda e: (e // 2, 0, 0)), whole_block((seq_len, rows)), whole_block((1, rows))),
        out_shape=(
            jax.ShapeDtypeStruct((count // 2, 2 * head_dim, seq_len), B16),
            jax.ShapeDtypeStruct((seq_len, rows), B16),
            jax.ShapeDtypeStruct((1, rows), F32),
        ),
        scratch_shapes=[pltpu.VMEM((rows, seq_len), F32), pltpu.VMEM((2 * head_dim, seq_len), F32)],
        compiler_params=pltpu.CompilerParams(vmem_limit_bytes=40 * MIB),
        cost_estimate=cost(3000),
        name='normed_grads',
    )(gathered, x_rows, wq_rows, wkv_rows, cos_t, sin_t)


def qkv_grad_kernel(width, head_dim, g_ref, dkv_ref, u_ref, dwq_ref, dwk_ref, dwv_ref):
    step = pl.program_id(0)
    dwq_ref[:] = jnp.dot(g_ref[0, :width, :], u_ref[:], preferred_element_type=F32).T
    kv_heads = dkv_ref.shape[0]

    @pl.when(step == 0)
    def _():
        both = jnp.dot(dkv_ref[:].reshape(kv_heads * 2 * head_dim, -1), u_ref[:], preferred_element_type=F32).T
        for out_ref, offset in ((dwk_ref, 0), (dwv_ref, head_dim)):
            out_ref[:] = jnp.concatenate([both[:, h * 2 * head_dim + offset:h * 2 * head_dim + offset + head_dim] for h in range(kv_heads)], axis=1)


def qkv_grads(gathered, dkv_t, u_rows, width, head_dim):
    count, height, seq_len = gathered.shape
    rows = u_rows.shape[1]
    kv_width = dkv_t.shape[0] * head_dim
    kv_spec = whole_block((rows, kv_width))
    return pl.pallas_call(
        functools.partial(qkv_grad_kernel, width, head_dim),
        grid=(count,),
        in_specs=[
            pl.BlockSpec((1, height, seq_len), lambda e: (e, 0, 0)),
            whole_block(dkv_t.shape),
            whole_block(u_rows.shape),
        ],
        out_specs=(pl.BlockSpec((rows, width), lambda e: (0, e)), kv_spec, kv_spec),
        out_shape=(
            jax.ShapeDtypeStruct((rows, count * width), F32),
            jax.ShapeDtypeStruct((rows, kv_width), F32),
            jax.ShapeDtypeStruct((rows, kv_width), F32),
        ),
        compiler_params=pltpu.CompilerParams(vmem_limit_bytes=40 * MIB),
        cost_estimate=cost(3000),
        name='qkv_grads',
    )(gathered, dkv_t, u_rows)


def solution(mesh):
    n_dev = mesh.shape['sp']
    gather_rows = functools.partial(lax.all_gather, axis_name='sp', axis=0, tiled=True)
    scatter_rows = functools.partial(lax.psum_scatter, axis_name='sp', scatter_dimension=0, tiled=True)
    swap_blocks = functools.partial(lax.all_to_all, axis_name='sp', split_axis=0, concat_axis=0, tiled=True)

    def send_blocks(others, order=XOR_ORDER):
        others = lax.optimization_barrier(tuple(with_layout_constraint(other, Layout((0, 1, 2))) for other in others))
        came = []
        for k, other in zip(order, others):
            came.append(with_layout_constraint(lax.ppermute(other, 'sp', [(i, i ^ k) for i in range(n_dev)]), Layout((0, 1, 2))))
        return came

    def pick_blocks(blocks):
        me = lax.axis_index('sp')
        return [lax.dynamic_index_in_dim(blocks, lax.bitwise_xor(me, k), axis=0, keepdims=True) for k in XOR_ORDER]

    def after(value, *others):
        return lax.optimization_barrier((value,) + others)[0]

    def to_tokens(columns):
        blocks = swap_blocks(columns.reshape(n_dev, -1, columns.shape[1]))
        return blocks.transpose(1, 0, 2).reshape(blocks.shape[1], -1)

    def layer_step(x_in, positions, d_out, norm1_gain, norm2_gain, w_q, w_k, w_v, w_o, w_gate, w_up, w_down):
        tokens, model_dim = x_in.shape
        rows = model_dim // n_dev
        seq_len = tokens * n_dev
        q_heads, head_dim = w_q.shape[1:]
        kv_heads = w_k.shape[1]
        heads = q_heads // n_dev
        width = heads * head_dim
        kv_repeat = n_dev // kv_heads
        ffn_part = w_down.shape[0]
        me = lax.axis_index('sp')
        own_rows = functools.partial(lax.dynamic_slice_in_dim, start_index=me * rows, slice_size=rows, axis=1)

        x_full = gather_rows(x_in)
        wq_rows = w_q.reshape(rows, q_heads * head_dim)
        wk_rows = w_k.reshape(rows, kv_heads * head_dim)
        wv_rows = w_v.reshape(rows, kv_heads * head_dim)
        wo_rows = w_o.reshape(width, model_dim)

        wq_blocks = wq_rows.reshape(rows, n_dev, width).transpose(1, 0, 2)
        wk_blocks = jnp.repeat(w_k.transpose(1, 0, 2), kv_repeat, axis=0)
        wv_blocks = jnp.repeat(w_v.transpose(1, 0, 2), kv_repeat, axis=0)
        qkv_blocks = jnp.concatenate([wq_blocks, wk_blocks, wv_blocks], axis=2)
        lane_width = qkv_blocks.shape[2]
        small = jnp.stack([norm1_gain, norm2_gain, (positions // 128).astype(B16), (positions % 128).astype(B16)])
        small = jnp.pad(small, ((0, 12), (0, lane_width - rows)))
        small = jnp.broadcast_to(small[None], (n_dev,) + small.shape)
        qkv_cols = swap_blocks(jnp.concatenate([qkv_blocks, small], axis=1))
        w_qkv = qkv_cols[:, :rows].reshape(model_dim, lane_width)
        gain1 = qkv_cols[:, rows, :rows].reshape(model_dim).astype(F32)
        gain2 = qkv_cols[:, rows + 1, :rows].reshape(model_dim).astype(F32)
        pos_all = (qkv_cols[:, rows + 2, :rows].astype(F32) * 128.0 + qkv_cols[:, rows + 3, :rows].astype(F32)).reshape(seq_len)

        wo_full = gather_rows(wo_rows)
        dy_full = gather_rows(d_out)
        gate_blocks = w_gate.reshape(rows, n_dev, ffn_part).transpose(1, 0, 2)
        up_blocks = w_up.reshape(rows, n_dev, ffn_part).transpose(1, 0, 2)
        gate_others, up_others = pick_blocks(gate_blocks), pick_blocks(up_blocks)
        gate_came = send_blocks(gate_others[:FIRST], XOR_ORDER[:FIRST])
        gate_others, up_others, x_full = lax.optimization_barrier((gate_others[FIRST:], up_others, x_full))
        gate_came, up_came = gate_came + send_blocks(gate_others, XOR_ORDER[FIRST:]), send_blocks(up_others)

        cos_tab, sin_tab = rope_tables(pos_all, head_dim)
        cos_tab, sin_tab = cos_tab[:, 0], sin_tab[:, 0]
        cos_lanes = jnp.tile(cos_tab, (1, 4))
        sin_lanes = jnp.tile(jnp.concatenate([-sin_tab, sin_tab], axis=1), (1, 2))
        q_rot, k_rot, v_lin, u_rows, x_rows = project_qkv(me, x_full, gain1[None], w_qkv, cos_lanes, sin_lanes, head_dim)
        attn_cols, row_max, inv_sum = attention_forward(q_rot, k_rot, v_lin, heads)
        attn_tok = to_tokens(attn_cols)
        hidden = (x_in.astype(F32) + jnp.dot(attn_tok, wo_full, preferred_element_type=F32)).astype(B16)
        h_full = gather_blocks(hidden, 1)
        wk_late, wv_late = lax.optimization_barrier((wk_rows, wv_rows, hidden))[:2]
        wkv_rows = pair_heads(wk_late, wv_late)
        weights = (gate_blocks, *gate_came, up_blocks, *up_came)
        mlp_in, gate_act, up_act, glu_out, y_part = mlp_call(
            mlp_forward_kernel, me, (h_full, gain2[None], w_down),
            [token_tile(model_dim), whole_block((1, model_dim)), whole_block(w_down.shape)],
            weights, (model_dim, ffn_part, ffn_part, ffn_part, model_dim), (B16, B16, B16, B16, F32), 18_000)
        y_sum = scatter_rows(y_part)
        d_gate_act, d_up_act, d_mlp_part = mlp_call(
            mlp_backward_kernel, me, (gate_act, up_act, dy_full, w_down),
            [token_tile(ffn_part), token_tile(ffn_part), token_tile(model_dim), whole_block(w_down.shape)],
            weights, (ffn_part, ffn_part, model_dim), (B16, B16, F32), 18_000)
        d_gate_blocks, d_up_blocks = ffn_grads(me, mlp_in, d_gate_act, d_up_act, n_dev)
        d_gate_others = [d_gate_blocks[k] for k in XOR_ORDER]
        d_up_others = [d_up_blocks[k] for k in XOR_ORDER]
        cos_t, sin_t = cos_tab.T, sin_tab.T
        d_mlp_part, d_up_others, d_gate_others, cos_t, sin_t, wkv_rows = lax.optimization_barrier((d_mlp_part, d_up_others, d_gate_others, cos_t, sin_t, wkv_rows))
        d_gate_came = send_blocks(d_gate_others[:NOW], XOR_ORDER[:NOW])
        d_mlp_sum = reduce_blocks(d_mlp_part, 4)
        d_mlp_in = d_mlp_sum.astype(B16).astype(F32)
        hidden_f = hidden.astype(F32)
        inv2 = inverse_rms(hidden_f)
        d_hidden = (d_out.astype(F32) + norm_backward(d_mlp_in, hidden_f, inv2, gain2)).astype(B16)
        d_g2_part = jnp.sum(d_mlp_in * hidden_f * inv2, axis=0)
        dh_full = gather_blocks(d_hidden, 2)
        d_gate_came += send_blocks(after(d_gate_others[NOW:], dh_full), XOR_ORDER[NOW:])
        d_up_came = send_blocks(after(d_up_others[:EARLY], dh_full), XOR_ORDER[:EARLY])

        d_attn = jnp.einsum('td,cd->tc', dh_full, wo_rows, preferred_element_type=F32).astype(B16)
        dq_t, dk_t, dv_t = attention_backward(q_rot, d_attn, k_rot, v_lin, row_max, inv_sum, cos_lanes, sin_lanes, heads)
        piece_hi = lax.reduce_precision(d_g2_part, 8, 7)
        piece_mid = lax.reduce_precision(d_g2_part - piece_hi, 8, 7)
        piece_lo = lax.reduce_precision(d_g2_part - piece_hi - piece_mid, 8, 7)
        pieces = jnp.pad(jnp.stack([piece_hi, piece_mid, piece_lo]).astype(B16), ((0, 13), (0, 0)))
        dqkv_t = gather_rows(jnp.concatenate([dq_t, dk_t, dv_t, pieces], axis=0)).reshape(n_dev, width + 2 * head_dim + 16, seq_len)
        d_g2 = jnp.sum(own_rows(dqkv_t[:, width + 2 * head_dim:width + 2 * head_dim + 3].reshape(-1, seq_len)).astype(F32), axis=0)
        glu_late, o_late = lax.optimization_barrier((glu_out, attn_cols, dk_t))[:2]
        d_down = jnp.einsum('tf,td->fd', glu_late, dy_full, preferred_element_type=F32)
        d_wo = jnp.einsum('tc,td->cd', o_late, dh_full, preferred_element_type=F32)
        d_gate = join_columns(me, d_gate_blocks[0], d_gate_came)
        dqkv_t, d_down, d_wo, d_gate = lax.optimization_barrier((dqkv_t, d_down, d_wo, d_gate))
        d_up_came += send_blocks(after(d_up_others[EARLY:], dqkv_t), XOR_ORDER[EARLY:])
        d_up = join_columns(me, d_up_blocks[0], d_up_came)
        y_out = (hidden_f + y_sum).astype(B16)

        dkv_t, d_norm_cols, d_g1 = normed_grads(dqkv_t, x_rows, wq_rows, wkv_rows, cos_t, sin_t, head_dim)
        d_wq, d_wk, d_wv = qkv_grads(dqkv_t, dkv_t, u_rows, width, head_dim)
        d_g1 = d_g1[0]
        d_normed = to_tokens(d_norm_cols).astype(F32)
        x_f32 = x_in.astype(F32)
        d_x = (d_hidden.astype(F32) + norm_backward(d_normed, x_f32, inverse_rms(x_f32), gain1)).astype(B16)
        return (y_out, d_x, d_g1, d_g2, d_wq.reshape(w_q.shape), d_wk.reshape(w_k.shape), d_wv.reshape(w_v.shape), d_wo.reshape(w_o.shape), d_gate, d_up, d_down)

    all_rows = P('sp')
    return jax.shard_map(layer_step, mesh=mesh, in_specs=(all_rows,) * 12, out_specs=(all_rows,) * 11, check_vma=False)
```

time: 898 us -> 830 us (0.924)
  waiting for transfers between devices: 518 us -> 242 us
  Pallas kernels: 200 us -> 421 us
  local copies, waits for them, and re-layouts: 79.1 us -> 65.7 us
    pallas_call x0 -> x4, Pallas kernels: none -> 217 us  [the longest x1 104 us: reduce_blocks(): pl.pallas_call(reduce_kernel, out_shape=jax.ShapeDtypeStruct((rows, cols)...]
    reduce_scatter x3 -> x1, waiting for transfers between devices: 135 us -> 0.02 us  [layer_step(): y_sum = scatter_rows(y_part)]
    ppermute x28, waiting for transfers between devices: 244 us -> 182 us  [send_blocks(): lax.ppermute(other, 'sp', [(i, i ^ k) for i in range(n_dev)])]
    all_gather x2 -> x0, waiting for transfers between devices: 52.9 us -> none  [the longest x1 48.7 us: layer_step(): dh_full = gather_rows(d_hidden)]
    all_to_all x2, waiting for transfers between devices: 37.1 us -> 0.01 us  [to_tokens(): blocks = swap_blocks(columns.reshape(n_dev, -1, columns.shape[1]))]
    all_gather x1, waiting for transfers between devices: 0.01 us -> 29.9 us  [layer_step(): gather_rows(jnp.concatenate([dq_t, dk_t, dv_t, pieces], axis=0))]
    all_gather x1, waiting for transfers between devices: 20.2 us -> 0.01 us  [layer_step(): dy_full = gather_rows(d_out)]
    unnamed x139 -> x135, local copies, waits for them, and re-layouts: 31.7 us -> 24.1 us
  transfers between devices with their start and end apart: 40 -> 36, of which waited for: 29 -> 18; matrix products, arithmetic and copies ran while one was open for 9% -> 10% of each run, Pallas kernels for 13% -> 40%
where the time goes in v2:
time: 830 us; the launch traced here: 822 us
  Pallas kernels  421 us (51%)
  waiting for transfers between devices  242 us (29%)
  local copies, waits for them, and re-layouts  65.7 us (8%)
  starting transfers between devices  33.9 us (4%)
  matrix products  28.8 us (3%)
  other arithmetic  15.7 us (2%)
  between operations  14.8 us (2%)
    ppermute x28, waiting for transfers between devices, send_blocks(): lax.ppermute(other, 'sp', [(i, i ^ k) for i in range(n_dev)])  182 us
    pallas_call x1, Pallas kernels, reduce_blocks(): pl.pallas_call(reduce_kernel, out_shape=jax.ShapeDtypeStruct((rows, cols)...  104 us
    pallas_call x2, Pallas kernels, gather_blocks(): pl.pallas_call(functools.partial(gather_kernel, split), out_shape=jax.Sha...  101 us
    pallas_call x2, Pallas kernels, mlp_call(): pl.pallas_call(kernel, grid_spec=pltpu.PrefetchScalarGridSpec(num_scalar_...  66.2 us
    pallas_call x1, Pallas kernels, attention_backward(): pl.pallas_call(functools.partial(attention_backward_kernel, heads, head_d...  48.3 us
    pallas_call x1, Pallas kernels, attention_forward(): pl.pallas_call(functools.partial(attention_forward_kernel, heads, head_di...  37.7 us
    all_gather x1, waiting for transfers between devices, layer_step(): gather_rows(jnp.concatenate([dq_t, dk_t, dv_t, pieces], axis=0))  29.9 us
    unnamed x135, local copies, waits for them, and re-layouts  24.1 us
  transfers between devices with their start and end apart: 36, of which 18 were waited for; matrix products, arithmetic and copies ran while one was open for 10% of the time, Pallas kernels for 40%

profile of v2, /device:TPU:0, one launch (start us, length us, event | category | flops | bytes accessed | tf_op | source)
XLA Modules:
  0.0 821.9 jit_solution(15477947034098402662)
XLA Ops:
  57.0 21.4 %all-gather.5.cloned.1.call-done.x_ref = bf16[2048,2048]{1,0:T(8,128)(2,1)} async-done(((bf16[256,2048]{1,0:T(8,128)(2,1)}), bf16[2048,2048]{1,0:T(8,128)(2,1)}) %all-gather.5.cloned.1.call-update) | async-done | bytes 8388624 | tf_op jit(solution)/shard_map/all_gather | solution.py:730
  83.1 8.8 %project_qkv.1 = (bf16[2048,256]{1,0:T(8,128)(2,1)S(1)}, bf16[2048,64]{1,0:T(8,128)(2,1)S(1)}, bf16[2048,64]{1,0:T(8,128)(2,1)S(1)}, bf16[2048,256]{1,0:T(8,128)(2,1)S(1)}, f32[2048,256]{1,0:T(8,128)S(1)}) custom-call(s32[1]{0:T(128)} %bitcast.me_ref, bf16[2048,2048]{1,0:T(8,128)(2,1)S(1)} %copy-done, f32[1,2048]{1,0:T(1,128)S(1)} %bitcast.66, ...), custom_call_target="tpu_custom_call" | custom-call | flops 3000000000 | bytes 20000000 | tf_op jit(solution)/shard_map/project_qkv/pallas_call | solution.py:429
  94.2 37.7 %attention_forward.1 = (bf16[2048,256]{1,0:T(8,128)(2,1)S(1)}, f32[8192,1]{1,0:T(8,128)}, f32[8192,1]{1,0:T(8,128)}) custom-call(bf16[2048,256]{1,0:T(8,128)(2,1)S(1)} %get-tuple-element.131.q_ref, bf16[2048,64]{1,0:T(8,128)(2,1)S(1)} %get-tuple-element.132.k_ref, bf16[2048,64]{1,0:T(8,128)(2,1)S(1)} %get-tuple-element.133.v_ref), custom_call_target="tpu_custom_call" | custom-call | flops 20000000000 | bytes 20000000 | tf_op jit(solution)/shard_map/attention_forward/pallas_call | solution.py:123
  152.5 17.3 %collective-permute-done.refs_1_ = bf16[1,256,704]{2,1,0:T(8,128)(2,1)} collective-permute-done((bf16[1,256,704]{2,1,0:T(8,128)(2,1)}, bf16[1,256,704]{2,1,0:T(8,128)(2,1)}, u32[]{:S(2)}, u32[]{:S(2)}) %collective-permute-start) | collective-permute-done | bytes 360480 | tf_op jit(solution)/shard_map/ppermute | solution.py:703
  171.5 12.7 %collective-permute-done.7.refs_9_ = bf16[1,256,704]{2,1,0:T(8,128)(2,1)} collective-permute-done((bf16[1,256,704]{2,1,0:T(8,128)(2,1)}, bf16[1,256,704]{2,1,0:T(8,128)(2,1)}, u32[]{:S(2)}, u32[]{:S(2)}) %collective-permute-start.7) | collective-permute-done | bytes 360480 | tf_op jit(solution)/shard_map/ppermute | solution.py:703
  193.3 8.6 %collective-permute-done.9.refs_11_ = bf16[1,256,704]{2,1,0:T(8,128)(2,1)S(1)} collective-permute-done((bf16[1,256,704]{2,1,0:T(8,128)(2,1)}, bf16[1,256,704]{2,1,0:T(8,128)(2,1)S(1)}, u32[]{:S(2)}, u32[]{:S(2)}) %collective-permute-start.9) | collective-permute-done | bytes 360480 | tf_op jit(solution)/shard_map/ppermute | solution.py:703
  202.0 14.9 %collective-permute-done.10.refs_12_ = bf16[1,256,704]{2,1,0:T(8,128)(2,1)S(1)} collective-permute-done((bf16[1,256,704]{2,1,0:T(8,128)(2,1)}, bf16[1,256,704]{2,1,0:T(8,128)(2,1)S(1)}, u32[]{:S(2)}, u32[]{:S(2)}) %collective-permute-start.10) | collective-permute-done | bytes 360480 | tf_op jit(solution)/shard_map/ppermute | solution.py:703
  227.1 60.6 %gather_blocks.2.h_ref = bf16[2048,2048]{1,0:T(8,128)(2,1)} custom-call(bf16[256,2048]{1,0:T(8,128)(2,1)} %get-tuple-element.295.src_ref), custom_call_target="tpu_custom_call" | custom-call | flops 30000001024 | bytes 20000000 | tf_op jit(solution)/shard_map/gather_blocks/pallas_call | solution.py:281
  288.5 29.1 %shard_map.203 = (bf16[2048,2048]{1,0:T(8,128)(2,1)}, bf16[2048,704]{1,0:T(8,128)(2,1)}, bf16[2048,704]{1,0:T(8,128)(2,1)}, bf16[2048,704]{1,0:T(8,128)(2,1)}, f32[2048,2048]{1,0:T(8,128)}) custom-call(s32[1]{0:T(128)} %bitcast.me_ref, bf16[2048,2048]{1,0:T(8,128)(2,1)} %gather_blocks.2.h_ref, f32[1,2048]{1,0:T(1,128)} %bitcast.116, ...), custom_call_target="tpu_custom_call" | custom-call | flops 17999998976 | bytes 20000000 | tf_op jit(solution)/shard_map/pallas_call | solution.py:501
  323.1 37.1 %shard_map.204 = (bf16[2048,704]{1,0:T(8,128)(2,1)}, bf16[2048,704]{1,0:T(8,128)(2,1)}, f32[2048,2048]{1,0:T(8,128)}) custom-call(s32[1]{0:T(128)} %bitcast.me_ref, bf16[2048,704]{1,0:T(8,128)(2,1)} %get-tuple-element.162.gate_ref, bf16[2048,704]{1,0:T(8,128)(2,1)} %get-tuple-element.163.up_ref, bf16[2048,2048]{1,0:T(8,128)(2,1)} %all-gather.9.cloned.1.call-done.dy_ref, ...), custom_call_target="tpu_custom_call" | custom-call | flops 17999998976 | bytes 20000000 | tf_op jit(solution)/shard_map/pallas_call | solution.py:501
  360.1 21.9 %ffn_grads.1 = (f32[1,704,256]{2,1,0:T(8,128)}, f32[1,704,256]{2,1,0:T(8,128)}, f32[1,704,256]{2,1,0:T(8,128)}, f32[1,704,256]{2,1,0:T(8,128)}, f32[1,704,256]{2...) custom-call(s32[1]{0:T(128)} %bitcast.me_ref, ...), custom_call_target="tpu_custom_call" | custom-call | flops 12000000000 | bytes 20000000 | tf_op jit(solution)/shard_map/ffn_grads/pallas_call | solution.py:537
  382.1 104.4 %reduce_blocks.1 = f32[256,2048]{1,0:T(8,128)S(1)} custom-call(f32[8,256,2048]{2,1,0:T(8,128)} %bitcast.121), custom_call_target="tpu_custom_call" | custom-call | flops 60000002048 | bytes 20000000 | tf_op jit(solution)/shard_map/reduce_blocks/pallas_call | solution.py:371
  491.3 40.8 %gather_blocks.3 = bf16[2048,2048]{1,0:T(8,128)(2,1)} custom-call(bf16[256,2048]{1,0:T(8,128)(2,1)} %get-tuple-element.280.src_ref), custom_call_target="tpu_custom_call" | custom-call | flops 30000001024 | bytes 20000000 | tf_op jit(solution)/shard_map/gather_blocks/pallas_call | solution.py:281
  538.1 48.3 %attention_backward.1 = (bf16[256,2048]{1,0:T(8,128)(2,1)S(1)}, bf16[64,2048]{1,0:T(8,128)(2,1)S(1)}, bf16[64,2048]{1,0:T(8,128)(2,1)S(1)}) custom-call(bf16[2048,256]{1,0:T(8,128)(2,1)S(1)} %copy-done.22, bf16[2048,256]{1,0:T(8,128)(2,1)S(1)} %convolution_convert_fusion.do_ref, bf16[2048,64]{1,0:T(8,128)(2,1)S(1)} %copy-done.24, ...), custom_call_target="tpu_custom_call" | custom-call | flops 40000000000 | bytes 20000000 | tf_op jit(solution)/shard_map/attention_backward/pallas_call | solution.py:200
  593.7 11.8 %fusion.29 = f32[704,2048]{1,0:T(8,128)} fusion(bf16[2048,704]{1,0:T(8,128)(2,1)} %get-tuple-element.191, bf16[2048,2048]{1,0:T(8,128)(2,1)} %all-gather.9.cloned.1.call-done.dy_ref), kind=kOutput, calls=%fused_computation.85 | convolution fusion | flops 5905580032 | bytes 17039360 | tf_op jit(solution)/shard_map/tf,td->fd/dot_general | solution.py:805
  605.5 13.8 %collective-permute-done.14.refs_1_ = f32[1,704,256]{2,1,0:T(8,128)S(1)} collective-permute-done((f32[1,704,256]{2,1,0:T(8,128)}, f32[1,704,256]{2,1,0:T(8,128)S(1)}, u32[]{:S(2)}, u32[]{:S(2)}) %collective-permute-start.14) | collective-permute-done | bytes 720928 | tf_op jit(solution)/shard_map/ppermute | solution.py:703
  623.8 17.7 %collective-permute-done.16.refs_3_ = f32[1,704,256]{2,1,0:T(8,128)S(1)} collective-permute-done((f32[1,704,256]{2,1,0:T(8,128)}, f32[1,704,256]{2,1,0:T(8,128)S(1)}, u32[]{:S(2)}, u32[]{:S(2)}) %collective-permute-start.16) | collective-permute-done | bytes 720928 | tf_op jit(solution)/shard_map/ppermute | solution.py:703
  642.1 17.8 %collective-permute-done.17.refs_4_ = f32[1,704,256]{2,1,0:T(8,128)S(1)} collective-permute-done((f32[1,704,256]{2,1,0:T(8,128)}, f32[1,704,256]{2,1,0:T(8,128)S(1)}, u32[]{:S(2)}, u32[]{:S(2)}) %collective-permute-start.17) | collective-permute-done | bytes 720928 | tf_op jit(solution)/shard_map/ppermute | solution.py:703
  663.7 27.1 %collective-permute-done.19.refs_6_ = f32[1,704,256]{2,1,0:T(8,128)S(1)} collective-permute-done((f32[1,704,256]{2,1,0:T(8,128)S(1)}, f32[1,704,256]{2,1,0:T(8,128)S(1)}, u32[]{:S(2)}, u32[]{:S(2)}) %collective-permute-start.19) | collective-permute-done | bytes 720928 | tf_op jit(solution)/shard_map/ppermute | solution.py:703
  695.0 29.9 %all-gather.11.cloned.1.call-done = bf16[3200,2048]{1,0:T(8,128)(2,1)} async-done(((bf16[400,2048]{1,0:T(8,128)(2,1)}), bf16[3200,2048]{1,0:T(8,128)(2,1)}) %all-gather.11.cloned.1.call-update) | async-done | bytes 13107216 | tf_op jit(solution)/shard_map/all_gather | solution.py:802
  726.8 11.5 %normed_grads.1 = (bf16[4,128,2048]{2,1,0:T(8,128)(2,1)S(1)}, bf16[2048,256]{1,0:T(8,128)(2,1)S(1)}, f32[1,256]{1,0:T(1,128)}) custom-call(bf16[8,400,2048]{2,1,0:T(8,128)(2,1)} %bitcast.69, f32[2048,256]{1,0:T(8,128)S(1)} %copy-done.7, bf16[256,2048]{1,0:T(8,128)(2,1)S(1)} %copy.158.wq_ref, bf16[256,512]{1,0:T(8,128)(2,1)S(1)} %copy-done.11, ...), custom_call_target="tpu_custom_call" | custom-call | flops 3000000000 | bytes 20000000 | tf_op jit(solution)/shard_map/normed_grads/pallas_call | solution.py:632
  752.6 9.8 %qkv_grads.1 = (f32[256,2048]{1,0:T(8,128)S(1)}, f32[256,256]{1,0:T(8,128)S(1)}, f32[256,256]{1,0:T(8,128)S(1)}) custom-call(bf16[8,400,2048]{2,1,0:T(8,128)(2,1)} %bitcast.71, bf16[4,128,2048]{2,1,0:T(8,128)(2,1)S(1)} %copy-done.9, bf16[2048,256]{1,0:T(8,128)(2,1)S(1)} %copy-done.13), custom_call_target="tpu_custom_call" | custom-call | flops 3000000000 | bytes 20000000 | tf_op jit(solution)/shard_map/qkv_grads/pallas_call | solution.py:673
  775.2 13.4 %collective-permute-done.24.refs_4_ = f32[1,704,256]{2,1,0:T(8,128)} collective-permute-done((f32[1,704,256]{2,1,0:T(8,128)}, f32[1,704,256]{2,1,0:T(8,128)}, u32[]{:S(2)}, u32[]{:S(2)}) %collective-permute-start.24) | collective-permute-done | bytes 720928 | tf_op jit(solution)/shard_map/ppermute | solution.py:703
  788.6 16.4 %collective-permute-done.26.refs_6_ = f32[1,704,256]{2,1,0:T(8,128)} collective-permute-done((f32[1,704,256]{2,1,0:T(8,128)}, f32[1,704,256]{2,1,0:T(8,128)}, u32[]{:S(2)}, u32[]{:S(2)}) %collective-permute-start.26) | collective-permute-done | bytes 720928 | tf_op jit(solution)/shard_map/ppermute | solution.py:703
  (269 shorter events, 174.2 us)
Async XLA Ops:
  7.2 71.2 %all-gather.5.cloned.1.call-start = ((), (), s32[]{:S(2)}) async-start(), calls=%async_computation.4 | async-start | bytes 9437184 | tf_op jit(solution)/shard_map/all_gather | solution.py:730
  8.0 177.8 %all-gather.7.cloned.1.call-start = ((), (), s32[]{:S(2)}) async-start(), calls=%async_computation.5 | async-start | bytes 9437184 | tf_op jit(solution)/shard_map/all_gather | solution.py:750
  8.7 314.3 %all-gather.9.cloned.1.call-start = ((), (), s32[]{:S(2)}) async-start(), calls=%async_computation.7 | async-start | bytes 9437184 | tf_op jit(solution)/shard_map/all_gather | solution.py:751
  133.2 52.6 %all-to-all-start.1 = ((bf16[8,256,256]{1,2,0:T(8,128)(2,1)}), bf16[8,256,256]{1,2,0:T(8,128)(2,1)}, u32[]{:S(2)}, u32[]{:S(2)}) async-start(bf16[8,256,256]{1,2,0:T(8,128)(2,1)} %copy.149), calls=%async_computation.1 | async-start | bytes 2097152 | tf_op jit(solution)/shard_map/all_to_all | solution.py:714
  136.2 351.1 %reduce-scatter.2.cloned.1.call-start = ((), (), s32[]{:S(2)}) async-start(), calls=%async_computation.6 | async-start | bytes 18874368 | tf_op jit(solution)/shard_map/reduce_scatter | solution.py:775
  149.7 52.2 %collective-permute-start.9 = (bf16[1,256,704]{2,1,0:T(8,128)(2,1)}, bf16[1,256,704]{2,1,0:T(8,128)(2,1)S(1)}, u32[]{:S(2)}, u32[]{:S(2)}) collective-permute-start(bf16[1,256,704]{2,1,0:T(8,128)(2,1)} %bitcast.107), channel_id=1, source_target_pairs={{0,6},{1,7},{2,4},{3,5},{4,2},{5,3},{6,0},{7,1}} | collective-permute-start | bytes 1081352 | tf_op jit(solution)/shard_map/ppermute | solution.py:703
  169.8 47.1 %collective-permute-start.10 = (bf16[1,256,704]{2,1,0:T(8,128)(2,1)}, bf16[1,256,704]{2,1,0:T(8,128)(2,1)S(1)}, u32[]{:S(2)}, u32[]{:S(2)}) collective-permute-start(bf16[1,256,704]{2,1,0:T(8,128)(2,1)} %bitcast.106), channel_id=1, source_target_pairs={{0,3},{1,2},{2,1},{3,0},{4,7},{5,6},{6,5},{7,4}} | collective-permute-start | bytes 1081352 | tf_op jit(solution)/shard_map/ppermute | solution.py:703
  170.2 47.2 %collective-permute-start.11 = (bf16[1,256,704]{2,1,0:T(8,128)(2,1)}, bf16[1,256,704]{2,1,0:T(8,128)(2,1)}, u32[]{:S(2)}, u32[]{:S(2)}) collective-permute-start(bf16[1,256,704]{2,1,0:T(8,128)(2,1)} %bitcast.105), channel_id=1, source_target_pairs={{0,5},{1,4},{2,7},{3,6},{4,1},{5,0},{6,3},{7,2}} | collective-permute-start | bytes 1081352 | tf_op jit(solution)/shard_map/ppermute | solution.py:703
  201.9 85.9 %collective-permute-start.2 = (bf16[1,256,704]{2,1,0:T(8,128)(2,1)S(1)}, bf16[1,256,704]{2,1,0:T(8,128)(2,1)}, u32[]{:S(2)}, u32[]{:S(2)}) collective-permute-start(bf16[1,256,704]{2,1,0:T(8,128)(2,1)S(1)} %bitcast.102), channel_id=1, source_target_pairs={{0,6},{1,7},{2,4},{3,5},{4,2},{5,3},{6,0},{7,1}} | collective-permute-start | bytes 1081352 | tf_op jit(solution)/shard_map/ppermute | solution.py:703
  216.9 70.9 %collective-permute-start.3 = (bf16[1,256,704]{2,1,0:T(8,128)(2,1)S(1)}, bf16[1,256,704]{2,1,0:T(8,128)(2,1)}, u32[]{:S(2)}, u32[]{:S(2)}) collective-permute-start(bf16[1,256,704]{2,1,0:T(8,128)(2,1)S(1)} %bitcast.101), channel_id=1, source_target_pairs={{0,3},{1,2},{2,1},{3,0},{4,7},{5,6},{6,5},{7,4}} | collective-permute-start | bytes 1081352 | tf_op jit(solution)/shard_map/ppermute | solution.py:703
  217.5 70.3 %collective-permute-start.4 = (bf16[1,256,704]{2,1,0:T(8,128)(2,1)S(1)}, bf16[1,256,704]{2,1,0:T(8,128)(2,1)}, u32[]{:S(2)}, u32[]{:S(2)}) collective-permute-start(bf16[1,256,704]{2,1,0:T(8,128)(2,1)S(1)} %bitcast.100), channel_id=1, source_target_pairs={{0,5},{1,4},{2,7},{3,6},{4,1},{5,0},{6,3},{7,2}} | collective-permute-start | bytes 1081352 | tf_op jit(solution)/shard_map/ppermute | solution.py:703
  226.5 61.3 %collective-permute-start.5 = (bf16[1,256,704]{2,1,0:T(8,128)(2,1)S(1)}, bf16[1,256,704]{2,1,0:T(8,128)(2,1)}, u32[]{:S(2)}, u32[]{:S(2)}) collective-permute-start(bf16[1,256,704]{2,1,0:T(8,128)(2,1)S(1)} %bitcast.99), channel_id=1, source_target_pairs={{0,7},{1,6},{2,5},{3,4},{4,3},{5,2},{6,1},{7,0}} | collective-permute-start | bytes 1081352 | tf_op jit(solution)/shard_map/ppermute | solution.py:703
  226.6 61.2 %collective-permute-start.6 = (bf16[1,256,704]{2,1,0:T(8,128)(2,1)S(1)}, bf16[1,256,704]{2,1,0:T(8,128)(2,1)S(1)}, u32[]{:S(2)}, u32[]{:S(2)}) collective-permute-start(bf16[1,256,704]{2,1,0:T(8,128)(2,1)S(1)} %bitcast.98), channel_id=1, source_target_pairs={{0,1},{1,0},{2,3},{3,2},{4,5},{5,4},{6,7},{7,6}} | collective-permute-start | bytes 1081352 | tf_op jit(solution)/shard_map/ppermute | solution.py:703
  317.7 407.2 %all-gather.11.cloned.1.call-start = ((), (), s32[]{:S(2)}) async-start(), calls=%async_computation.8 | async-start | bytes 14745600 | tf_op jit(solution)/shard_map/all_gather | solution.py:802
  590.5 51.0 %collective-permute-start.16 = (f32[1,704,256]{2,1,0:T(8,128)}, f32[1,704,256]{2,1,0:T(8,128)S(1)}, u32[]{:S(2)}, u32[]{:S(2)}) collective-permute-start(f32[1,704,256]{2,1,0:T(8,128)} %get-tuple-element.199), channel_id=1, source_target_pairs={{0,6},{1,7},{2,4},{3,5},{4,2},{5,3},{6,0},{7,1}} | collective-permute-start | bytes 2162696 | tf_op jit(solution)/shard_map/ppermute | solution.py:703
  592.1 67.9 %collective-permute-start.17 = (f32[1,704,256]{2,1,0:T(8,128)}, f32[1,704,256]{2,1,0:T(8,128)S(1)}, u32[]{:S(2)}, u32[]{:S(2)}) collective-permute-start(f32[1,704,256]{2,1,0:T(8,128)} %get-tuple-element.208), channel_id=1, source_target_pairs={{0,3},{1,2},{2,1},{3,0},{4,7},{5,6},{6,5},{7,4}} | collective-permute-start | bytes 2162696 | tf_op jit(solution)/shard_map/ppermute | solution.py:703
  592.4 71.2 %collective-permute-start.18 = (f32[1,704,256]{2,1,0:T(8,128)S(1)}, f32[1,704,256]{2,1,0:T(8,128)S(1)}, u32[]{:S(2)}, u32[]{:S(2)}) collective-permute-start(f32[1,704,256]{2,1,0:T(8,128)S(1)} %copy-done.58), channel_id=1, source_target_pairs={{0,5},{1,4},{2,7},{3,6},{4,1},{5,0},{6,3},{7,2}} | collective-permute-start | bytes 2162696 | tf_op jit(solution)/shard_map/ppermute | solution.py:703
  619.3 71.4 %collective-permute-start.19 = (f32[1,704,256]{2,1,0:T(8,128)S(1)}, f32[1,704,256]{2,1,0:T(8,128)S(1)}, u32[]{:S(2)}, u32[]{:S(2)}) collective-permute-start(f32[1,704,256]{2,1,0:T(8,128)S(1)} %copy-done.57), channel_id=1, source_target_pairs={{0,7},{1,6},{2,5},{3,4},{4,3},{5,2},{6,1},{7,0}} | collective-permute-start | bytes 2162696 | tf_op jit(solution)/shard_map/ppermute | solution.py:703
  623.8 66.9 %collective-permute-start.20 = (f32[1,704,256]{2,1,0:T(8,128)S(1)}, f32[1,704,256]{2,1,0:T(8,128)S(1)}, u32[]{:S(2)}, u32[]{:S(2)}) collective-permute-start(f32[1,704,256]{2,1,0:T(8,128)S(1)} %copy-done.56), channel_id=1, source_target_pairs={{0,1},{1,0},{2,3},{3,2},{4,5},{5,4},{6,7},{7,6}} | collective-permute-start | bytes 2162696 | tf_op jit(solution)/shard_map/ppermute | solution.py:703
  641.5 105.5 %collective-permute-start.21 = (f32[1,704,256]{2,1,0:T(8,128)}, f32[1,704,256]{2,1,0:T(8,128)}, u32[]{:S(2)}, u32[]{:S(2)}) collective-permute-start(f32[1,704,256]{2,1,0:T(8,128)} %get-tuple-element.233), channel_id=1, source_target_pairs={{0,2},{1,3},{2,0},{3,1},{4,6},{5,7},{6,4},{7,5}} | collective-permute-start | bytes 2162696 | tf_op jit(solution)/shard_map/ppermute | solution.py:703
  660.0 89.3 %collective-permute-start.22 = (f32[1,704,256]{2,1,0:T(8,128)}, f32[1,704,256]{2,1,0:T(8,128)}, u32[]{:S(2)}, u32[]{:S(2)}) collective-permute-start(f32[1,704,256]{2,1,0:T(8,128)} %get-tuple-element.234), channel_id=1, source_target_pairs={{0,4},{1,5},{2,6},{3,7},{4,0},{5,1},{6,2},{7,3}} | collective-permute-start | bytes 2162696 | tf_op jit(solution)/shard_map/ppermute | solution.py:703
  740.6 69.6 %all-to-all-start.2 = ((bf16[8,256,256]{2,1,0:T(8,128)(2,1)}), bf16[8,256,256]{2,1,0:T(8,128)(2,1)}, u32[]{:S(2)}, u32[]{:S(2)}) async-start(bf16[8,256,256]{2,1,0:T(8,128)(2,1)} %bitcast.65), calls=%async_computation.3 | async-start | bytes 2097152 | tf_op jit(solution)/shard_map/all_to_all | solution.py:714
  747.0 58.0 %collective-permute-start.26 = (f32[1,704,256]{2,1,0:T(8,128)}, f32[1,704,256]{2,1,0:T(8,128)}, u32[]{:S(2)}, u32[]{:S(2)}) collective-permute-start(f32[1,704,256]{2,1,0:T(8,128)} %get-tuple-element.246), channel_id=1, source_target_pairs={{0,7},{1,6},{2,5},{3,4},{4,3},{5,2},{6,1},{7,0}} | collective-permute-start | bytes 2162696 | tf_op jit(solution)/shard_map/ppermute | solution.py:703
  749.2 55.7 %collective-permute-start.27 = (f32[1,704,256]{2,1,0:T(8,128)}, f32[1,704,256]{2,1,0:T(8,128)}, u32[]{:S(2)}, u32[]{:S(2)}) collective-permute-start(f32[1,704,256]{2,1,0:T(8,128)} %get-tuple-element.247), channel_id=1, source_target_pairs={{0,1},{1,0},{2,3},{3,2},{4,5},{5,4},{6,7},{7,6}} | collective-permute-start | bytes 2162696 | tf_op jit(solution)/shard_map/ppermute | solution.py:703
  (78 other events, 1801.1 us)
Sparse Core Ops, SparseCore 0:
  9.9 68.5 all-gather.4
  80.3 48.6 all-gather.6
  130.8 88.8 all-gather.8
  317.8 136.6 reduce-scatter.1
  587.9 136.9 all-gather.10

commit v3 on v2

--- a/solution.py
+++ b/solution.py
@@ -11,7 +11,7 @@
 NORM_EPS = 1e-5
 NEG_LARGE = -1e30
 BLOCK = 256
-MLP_BLOCK = 512
+MLP_BLOCK = 256
 MIB = 1024 * 1024
 EARLY = 3
 NOW = 3
@@ -523,11 +523,13 @@
         da_t[:] = da_ref[:].T
         db_t[:] = db_ref[:].T
 
+    gate_grad = jnp.dot(da_t[:], m_ref[:], preferred_element_type=F32)
+    up_grad = jnp.dot(db_t[:], m_ref[:], preferred_element_type=F32)
     for k in range(count):
         @pl.when(step == k)
         def _():
-            out_refs[k][0] = jnp.dot(da_t[:], m_ref[:], preferred_element_type=F32)
-            out_refs[count + k][0] = jnp.dot(db_t[:], m_ref[:], preferred_element_type=F32)
+            out_refs[k][0] = gate_grad
+            out_refs[count + k][0] = up_grad
 
 
 def ffn_grads(me, mlp_in, d_gate_act, d_up_act, count):

time: 830 us -> 830 us (level)
  no operation moved by 1% of the time
where the time goes in v3:
time: 830 us; the launch traced here: 822 us
  Pallas kernels  421 us (51%)
  waiting for transfers between devices  242 us (29%)
  local copies, waits for them, and re-layouts  65.7 us (8%)
  starting transfers between devices  34.4 us (4%)
  matrix products  28.9 us (3%)
  other arithmetic  15.7 us (2%)
  between operations  14.9 us (2%)
    ppermute x28, waiting for transfers between devices, send_blocks(): lax.ppermute(other, 'sp', [(i, i ^ k) for i in range(n_dev)])  182 us
    pallas_call x1, Pallas kernels, reduce_blocks(): pl.pallas_call(reduce_kernel, out_shape=jax.ShapeDtypeStruct((rows, cols)...  102 us
    pallas_call x2, Pallas kernels, gather_blocks(): pl.pallas_call(functools.partial(gather_kernel, split), out_shape=jax.Sha...  101 us
    pallas_call x2, Pallas kernels, mlp_call(): pl.pallas_call(kernel, grid_spec=pltpu.PrefetchScalarGridSpec(num_scalar_...  65.7 us
    pallas_call x1, Pallas kernels, attention_backward(): pl.pallas_call(functools.partial(attention_backward_kernel, heads, head_d...  48.5 us
    pallas_call x1, Pallas kernels, attention_forward(): pl.pallas_call(functools.partial(attention_forward_kernel, heads, head_di...  37.7 us
    all_gather x1, waiting for transfers between devices, layer_step(): gather_rows(jnp.concatenate([dq_t, dk_t, dv_t, pieces], axis=0))  29.9 us
    unnamed x135, local copies, waits for them, and re-layouts  24.1 us
  transfers between devices with their start and end apart: 36, of which 18 were waited for; matrix products, arithmetic and copies ran while one was open for 10% of the time, Pallas kernels for 40%

profile of v3, /device:TPU:0, one launch (start us, length us, event | category | flops | bytes accessed | tf_op | source)
XLA Modules:
  0.0 822.2 jit_solution(17331315574016178892)
XLA Ops:
  57.0 21.4 %all-gather.5.cloned.1.call-done.x_ref = bf16[2048,2048]{1,0:T(8,128)(2,1)} async-done(((bf16[256,2048]{1,0:T(8,128)(2,1)}), bf16[2048,2048]{1,0:T(8,128)(2,1)}) %all-gather.5.cloned.1.call-update) | async-done | bytes 8388624 | tf_op jit(solution)/shard_map/all_gather | solution.py:732
  83.1 8.8 %project_qkv.1 = (bf16[2048,256]{1,0:T(8,128)(2,1)S(1)}, bf16[2048,64]{1,0:T(8,128)(2,1)S(1)}, bf16[2048,64]{1,0:T(8,128)(2,1)S(1)}, bf16[2048,256]{1,0:T(8,128)(2,1)S(1)}, f32[2048,256]{1,0:T(8,128)S(1)}) custom-call(s32[1]{0:T(128)} %bitcast.me_ref, bf16[2048,2048]{1,0:T(8,128)(2,1)S(1)} %copy-done, f32[1,2048]{1,0:T(1,128)S(1)} %bitcast.66, ...), custom_call_target="tpu_custom_call" | custom-call | flops 3000000000 | bytes 20000000 | tf_op jit(solution)/shard_map/project_qkv/pallas_call | solution.py:429
  94.2 37.7 %attention_forward.1 = (bf16[2048,256]{1,0:T(8,128)(2,1)S(1)}, f32[8192,1]{1,0:T(8,128)}, f32[8192,1]{1,0:T(8,128)}) custom-call(bf16[2048,256]{1,0:T(8,128)(2,1)S(1)} %get-tuple-element.131.q_ref, bf16[2048,64]{1,0:T(8,128)(2,1)S(1)} %get-tuple-element.132.k_ref, bf16[2048,64]{1,0:T(8,128)(2,1)S(1)} %get-tuple-element.133.v_ref), custom_call_target="tpu_custom_call" | custom-call | flops 20000000000 | bytes 20000000 | tf_op jit(solution)/shard_map/attention_forward/pallas_call | solution.py:123
  152.9 16.9 %collective-permute-done.refs_1_ = bf16[1,256,704]{2,1,0:T(8,128)(2,1)} collective-permute-done((bf16[1,256,704]{2,1,0:T(8,128)(2,1)}, bf16[1,256,704]{2,1,0:T(8,128)(2,1)}, u32[]{:S(2)}, u32[]{:S(2)}) %collective-permute-start) | collective-permute-done | bytes 360480 | tf_op jit(solution)/shard_map/ppermute | solution.py:705
  171.5 12.7 %collective-permute-done.7.refs_9_ = bf16[1,256,704]{2,1,0:T(8,128)(2,1)} collective-permute-done((bf16[1,256,704]{2,1,0:T(8,128)(2,1)}, bf16[1,256,704]{2,1,0:T(8,128)(2,1)}, u32[]{:S(2)}, u32[]{:S(2)}) %collective-permute-start.7) | collective-permute-done | bytes 360480 | tf_op jit(solution)/shard_map/ppermute | solution.py:705
  193.3 8.6 %collective-permute-done.9.refs_11_ = bf16[1,256,704]{2,1,0:T(8,128)(2,1)S(1)} collective-permute-done((bf16[1,256,704]{2,1,0:T(8,128)(2,1)}, bf16[1,256,704]{2,1,0:T(8,128)(2,1)S(1)}, u32[]{:S(2)}, u32[]{:S(2)}) %collective-permute-start.9) | collective-permute-done | bytes 360480 | tf_op jit(solution)/shard_map/ppermute | solution.py:705
  202.0 14.9 %collective-permute-done.10.refs_12_ = bf16[1,256,704]{2,1,0:T(8,128)(2,1)S(1)} collective-permute-done((bf16[1,256,704]{2,1,0:T(8,128)(2,1)}, bf16[1,256,704]{2,1,0:T(8,128)(2,1)S(1)}, u32[]{:S(2)}, u32[]{:S(2)}) %collective-permute-start.10) | collective-permute-done | bytes 360480 | tf_op jit(solution)/shard_map/ppermute | solution.py:705
  227.1 60.6 %gather_blocks.2.h_ref = bf16[2048,2048]{1,0:T(8,128)(2,1)} custom-call(bf16[256,2048]{1,0:T(8,128)(2,1)} %get-tuple-element.295.src_ref), custom_call_target="tpu_custom_call" | custom-call | flops 30000001024 | bytes 20000000 | tf_op jit(solution)/shard_map/gather_blocks/pallas_call | solution.py:281
  288.5 29.2 %shard_map.203 = (bf16[2048,2048]{1,0:T(8,128)(2,1)}, bf16[2048,704]{1,0:T(8,128)(2,1)}, bf16[2048,704]{1,0:T(8,128)(2,1)}, bf16[2048,704]{1,0:T(8,128)(2,1)}, f32[2048,2048]{1,0:T(8,128)}) custom-call(s32[1]{0:T(128)} %bitcast.me_ref, bf16[2048,2048]{1,0:T(8,128)(2,1)} %gather_blocks.2.h_ref, f32[1,2048]{1,0:T(1,128)} %bitcast.116, ...), custom_call_target="tpu_custom_call" | custom-call | flops 17999998976 | bytes 20000000 | tf_op jit(solution)/shard_map/pallas_call | solution.py:501
  323.1 36.4 %shard_map.204 = (bf16[2048,704]{1,0:T(8,128)(2,1)}, bf16[2048,704]{1,0:T(8,128)(2,1)}, f32[2048,2048]{1,0:T(8,128)}) custom-call(s32[1]{0:T(128)} %bitcast.me_ref, bf16[2048,704]{1,0:T(8,128)(2,1)} %get-tuple-element.162.gate_ref, bf16[2048,704]{1,0:T(8,128)(2,1)} %get-tuple-element.163.up_ref, bf16[2048,2048]{1,0:T(8,128)(2,1)} %all-gather.9.cloned.1.call-done.dy_ref, ...), custom_call_target="tpu_custom_call" | custom-call | flops 17999998976 | bytes 20000000 | tf_op jit(solution)/shard_map/pallas_call | solution.py:501
  359.6 24.1 %ffn_grads.1 = (f32[1,704,256]{2,1,0:T(8,128)}, f32[1,704,256]{2,1,0:T(8,128)}, f32[1,704,256]{2,1,0:T(8,128)}, f32[1,704,256]{2,1,0:T(8,128)}, f32[1,704,256]{2...) custom-call(s32[1]{0:T(128)} %bitcast.me_ref, ...), custom_call_target="tpu_custom_call" | custom-call | flops 12000000000 | bytes 20000000 | tf_op jit(solution)/shard_map/ffn_grads/pallas_call | solution.py:539
  383.7 102.4 %reduce_blocks.1 = f32[256,2048]{1,0:T(8,128)S(1)} custom-call(f32[8,256,2048]{2,1,0:T(8,128)} %bitcast.121), custom_call_target="tpu_custom_call" | custom-call | flops 60000002048 | bytes 20000000 | tf_op jit(solution)/shard_map/reduce_blocks/pallas_call | solution.py:371
  490.9 40.8 %gather_blocks.3 = bf16[2048,2048]{1,0:T(8,128)(2,1)} custom-call(bf16[256,2048]{1,0:T(8,128)(2,1)} %get-tuple-element.280.src_ref), custom_call_target="tpu_custom_call" | custom-call | flops 30000001024 | bytes 20000000 | tf_op jit(solution)/shard_map/gather_blocks/pallas_call | solution.py:281
  537.7 48.5 %attention_backward.1 = (bf16[256,2048]{1,0:T(8,128)(2,1)S(1)}, bf16[64,2048]{1,0:T(8,128)(2,1)S(1)}, bf16[64,2048]{1,0:T(8,128)(2,1)S(1)}) custom-call(bf16[2048,256]{1,0:T(8,128)(2,1)S(1)} %copy-done.22, bf16[2048,256]{1,0:T(8,128)(2,1)S(1)} %convolution_convert_fusion.do_ref, bf16[2048,64]{1,0:T(8,128)(2,1)S(1)} %copy-done.24, ...), custom_call_target="tpu_custom_call" | custom-call | flops 40000000000 | bytes 20000000 | tf_op jit(solution)/shard_map/attention_backward/pallas_call | solution.py:200
  593.5 11.8 %fusion.29 = f32[704,2048]{1,0:T(8,128)} fusion(bf16[2048,704]{1,0:T(8,128)(2,1)} %get-tuple-element.191, bf16[2048,2048]{1,0:T(8,128)(2,1)} %all-gather.9.cloned.1.call-done.dy_ref), kind=kOutput, calls=%fused_computation.85 | convolution fusion | flops 5905580032 | bytes 17039360 | tf_op jit(solution)/shard_map/tf,td->fd/dot_general | solution.py:807
  605.3 13.8 %collective-permute-done.14.refs_1_ = f32[1,704,256]{2,1,0:T(8,128)S(1)} collective-permute-done((f32[1,704,256]{2,1,0:T(8,128)}, f32[1,704,256]{2,1,0:T(8,128)S(1)}, u32[]{:S(2)}, u32[]{:S(2)}) %collective-permute-start.14) | collective-permute-done | bytes 720928 | tf_op jit(solution)/shard_map/ppermute | solution.py:705
  623.9 17.5 %collective-permute-done.16.refs_3_ = f32[1,704,256]{2,1,0:T(8,128)S(1)} collective-permute-done((f32[1,704,256]{2,1,0:T(8,128)}, f32[1,704,256]{2,1,0:T(8,128)S(1)}, u32[]{:S(2)}, u32[]{:S(2)}) %collective-permute-start.16) | collective-permute-done | bytes 720928 | tf_op jit(solution)/shard_map/ppermute | solution.py:705
  641.9 18.2 %collective-permute-done.17.refs_4_ = f32[1,704,256]{2,1,0:T(8,128)S(1)} collective-permute-done((f32[1,704,256]{2,1,0:T(8,128)}, f32[1,704,256]{2,1,0:T(8,128)S(1)}, u32[]{:S(2)}, u32[]{:S(2)}) %collective-permute-start.17) | collective-permute-done | bytes 720928 | tf_op jit(solution)/shard_map/ppermute | solution.py:705
  663.8 27.1 %collective-permute-done.19.refs_6_ = f32[1,704,256]{2,1,0:T(8,128)S(1)} collective-permute-done((f32[1,704,256]{2,1,0:T(8,128)S(1)}, f32[1,704,256]{2,1,0:T(8,128)S(1)}, u32[]{:S(2)}, u32[]{:S(2)}) %collective-permute-start.19) | collective-permute-done | bytes 720928 | tf_op jit(solution)/shard_map/ppermute | solution.py:705
  694.9 29.9 %all-gather.11.cloned.1.call-done = bf16[3200,2048]{1,0:T(8,128)(2,1)} async-done(((bf16[400,2048]{1,0:T(8,128)(2,1)}), bf16[3200,2048]{1,0:T(8,128)(2,1)}) %all-gather.11.cloned.1.call-update) | async-done | bytes 13107216 | tf_op jit(solution)/shard_map/all_gather | solution.py:804
  726.8 11.5 %normed_grads.1 = (bf16[4,128,2048]{2,1,0:T(8,128)(2,1)S(1)}, bf16[2048,256]{1,0:T(8,128)(2,1)S(1)}, f32[1,256]{1,0:T(1,128)}) custom-call(bf16[8,400,2048]{2,1,0:T(8,128)(2,1)} %bitcast.69, f32[2048,256]{1,0:T(8,128)S(1)} %copy-done.7, bf16[256,2048]{1,0:T(8,128)(2,1)S(1)} %copy.158.wq_ref, bf16[256,512]{1,0:T(8,128)(2,1)S(1)} %copy-done.11, ...), custom_call_target="tpu_custom_call" | custom-call | flops 3000000000 | bytes 20000000 | tf_op jit(solution)/shard_map/normed_grads/pallas_call | solution.py:634
  752.9 9.8 %qkv_grads.1 = (f32[256,2048]{1,0:T(8,128)S(1)}, f32[256,256]{1,0:T(8,128)S(1)}, f32[256,256]{1,0:T(8,128)S(1)}) custom-call(bf16[8,400,2048]{2,1,0:T(8,128)(2,1)} %bitcast.71, bf16[4,128,2048]{2,1,0:T(8,128)(2,1)S(1)} %copy-done.9, bf16[2048,256]{1,0:T(8,128)(2,1)S(1)} %copy-done.13), custom_call_target="tpu_custom_call" | custom-call | flops 3000000000 | bytes 20000000 | tf_op jit(solution)/shard_map/qkv_grads/pallas_call | solution.py:675
  775.4 13.4 %collective-permute-done.24.refs_4_ = f32[1,704,256]{2,1,0:T(8,128)} collective-permute-done((f32[1,704,256]{2,1,0:T(8,128)}, f32[1,704,256]{2,1,0:T(8,128)}, u32[]{:S(2)}, u32[]{:S(2)}) %collective-permute-start.24) | collective-permute-done | bytes 720928 | tf_op jit(solution)/shard_map/ppermute | solution.py:705
  788.8 16.4 %collective-permute-done.26.refs_6_ = f32[1,704,256]{2,1,0:T(8,128)} collective-permute-done((f32[1,704,256]{2,1,0:T(8,128)}, f32[1,704,256]{2,1,0:T(8,128)}, u32[]{:S(2)}, u32[]{:S(2)}) %collective-permute-start.26) | collective-permute-done | bytes 720928 | tf_op jit(solution)/shard_map/ppermute | solution.py:705
  (269 shorter events, 174.7 us)
Async XLA Ops:
  7.2 71.2 %all-gather.5.cloned.1.call-start = ((), (), s32[]{:S(2)}) async-start(), calls=%async_computation.4 | async-start | bytes 9437184 | tf_op jit(solution)/shard_map/all_gather | solution.py:732
  8.0 177.8 %all-gather.7.cloned.1.call-start = ((), (), s32[]{:S(2)}) async-start(), calls=%async_computation.5 | async-start | bytes 9437184 | tf_op jit(solution)/shard_map/all_gather | solution.py:752
  8.7 314.4 %all-gather.9.cloned.1.call-start = ((), (), s32[]{:S(2)}) async-start(), calls=%async_computation.7 | async-start | bytes 9437184 | tf_op jit(solution)/shard_map/all_gather | solution.py:753
  133.2 52.6 %all-to-all-start.1 = ((bf16[8,256,256]{1,2,0:T(8,128)(2,1)}), bf16[8,256,256]{1,2,0:T(8,128)(2,1)}, u32[]{:S(2)}, u32[]{:S(2)}) async-start(bf16[8,256,256]{1,2,0:T(8,128)(2,1)} %copy.149), calls=%async_computation.1 | async-start | bytes 2097152 | tf_op jit(solution)/shard_map/all_to_all | solution.py:716
  136.2 350.7 %reduce-scatter.2.cloned.1.call-start = ((), (), s32[]{:S(2)}) async-start(), calls=%async_computation.6 | async-start | bytes 18874368 | tf_op jit(solution)/shard_map/reduce_scatter | solution.py:777
  150.1 51.8 %collective-permute-start.9 = (bf16[1,256,704]{2,1,0:T(8,128)(2,1)}, bf16[1,256,704]{2,1,0:T(8,128)(2,1)S(1)}, u32[]{:S(2)}, u32[]{:S(2)}) collective-permute-start(bf16[1,256,704]{2,1,0:T(8,128)(2,1)} %bitcast.107), channel_id=1, source_target_pairs={{0,6},{1,7},{2,4},{3,5},{4,2},{5,3},{6,0},{7,1}} | collective-permute-start | bytes 1081352 | tf_op jit(solution)/shard_map/ppermute | solution.py:705
  169.8 47.1 %collective-permute-start.10 = (bf16[1,256,704]{2,1,0:T(8,128)(2,1)}, bf16[1,256,704]{2,1,0:T(8,128)(2,1)S(1)}, u32[]{:S(2)}, u32[]{:S(2)}) collective-permute-start(bf16[1,256,704]{2,1,0:T(8,128)(2,1)} %bitcast.106), channel_id=1, source_target_pairs={{0,3},{1,2},{2,1},{3,0},{4,7},{5,6},{6,5},{7,4}} | collective-permute-start | bytes 1081352 | tf_op jit(solution)/shard_map/ppermute | solution.py:705
  170.2 47.2 %collective-permute-start.11 = (bf16[1,256,704]{2,1,0:T(8,128)(2,1)}, bf16[1,256,704]{2,1,0:T(8,128)(2,1)}, u32[]{:S(2)}, u32[]{:S(2)}) collective-permute-start(bf16[1,256,704]{2,1,0:T(8,128)(2,1)} %bitcast.105), channel_id=1, source_target_pairs={{0,5},{1,4},{2,7},{3,6},{4,1},{5,0},{6,3},{7,2}} | collective-permute-start | bytes 1081352 | tf_op jit(solution)/shard_map/ppermute | solution.py:705
  201.9 85.9 %collective-permute-start.2 = (bf16[1,256,704]{2,1,0:T(8,128)(2,1)S(1)}, bf16[1,256,704]{2,1,0:T(8,128)(2,1)}, u32[]{:S(2)}, u32[]{:S(2)}) collective-permute-start(bf16[1,256,704]{2,1,0:T(8,128)(2,1)S(1)} %bitcast.102), channel_id=1, source_target_pairs={{0,6},{1,7},{2,4},{3,5},{4,2},{5,3},{6,0},{7,1}} | collective-permute-start | bytes 1081352 | tf_op jit(solution)/shard_map/ppermute | solution.py:705
  216.9 70.9 %collective-permute-start.3 = (bf16[1,256,704]{2,1,0:T(8,128)(2,1)S(1)}, bf16[1,256,704]{2,1,0:T(8,128)(2,1)}, u32[]{:S(2)}, u32[]{:S(2)}) collective-permute-start(bf16[1,256,704]{2,1,0:T(8,128)(2,1)S(1)} %bitcast.101), channel_id=1, source_target_pairs={{0,3},{1,2},{2,1},{3,0},{4,7},{5,6},{6,5},{7,4}} | collective-permute-start | bytes 1081352 | tf_op jit(solution)/shard_map/ppermute | solution.py:705
  217.5 70.3 %collective-permute-start.4 = (bf16[1,256,704]{2,1,0:T(8,128)(2,1)S(1)}, bf16[1,256,704]{2,1,0:T(8,128)(2,1)}, u32[]{:S(2)}, u32[]{:S(2)}) collective-permute-start(bf16[1,256,704]{2,1,0:T(8,128)(2,1)S(1)} %bitcast.100), channel_id=1, source_target_pairs={{0,5},{1,4},{2,7},{3,6},{4,1},{5,0},{6,3},{7,2}} | collective-permute-start | bytes 1081352 | tf_op jit(solution)/shard_map/ppermute | solution.py:705
  226.5 61.3 %collective-permute-start.5 = (bf16[1,256,704]{2,1,0:T(8,128)(2,1)S(1)}, bf16[1,256,704]{2,1,0:T(8,128)(2,1)}, u32[]{:S(2)}, u32[]{:S(2)}) collective-permute-start(bf16[1,256,704]{2,1,0:T(8,128)(2,1)S(1)} %bitcast.99), channel_id=1, source_target_pairs={{0,7},{1,6},{2,5},{3,4},{4,3},{5,2},{6,1},{7,0}} | collective-permute-start | bytes 1081352 | tf_op jit(solution)/shard_map/ppermute | solution.py:705
  226.6 61.2 %collective-permute-start.6 = (bf16[1,256,704]{2,1,0:T(8,128)(2,1)S(1)}, bf16[1,256,704]{2,1,0:T(8,128)(2,1)S(1)}, u32[]{:S(2)}, u32[]{:S(2)}) collective-permute-start(bf16[1,256,704]{2,1,0:T(8,128)(2,1)S(1)} %bitcast.98), channel_id=1, source_target_pairs={{0,1},{1,0},{2,3},{3,2},{4,5},{5,4},{6,7},{7,6}} | collective-permute-start | bytes 1081352 | tf_op jit(solution)/shard_map/ppermute | solution.py:705
  317.8 407.0 %all-gather.11.cloned.1.call-start = ((), (), s32[]{:S(2)}) async-start(), calls=%async_computation.8 | async-start | bytes 14745600 | tf_op jit(solution)/shard_map/all_gather | solution.py:804
  590.3 51.1 %collective-permute-start.16 = (f32[1,704,256]{2,1,0:T(8,128)}, f32[1,704,256]{2,1,0:T(8,128)S(1)}, u32[]{:S(2)}, u32[]{:S(2)}) collective-permute-start(f32[1,704,256]{2,1,0:T(8,128)} %get-tuple-element.199), channel_id=1, source_target_pairs={{0,6},{1,7},{2,4},{3,5},{4,2},{5,3},{6,0},{7,1}} | collective-permute-start | bytes 2162696 | tf_op jit(solution)/shard_map/ppermute | solution.py:705
  591.9 68.2 %collective-permute-start.17 = (f32[1,704,256]{2,1,0:T(8,128)}, f32[1,704,256]{2,1,0:T(8,128)S(1)}, u32[]{:S(2)}, u32[]{:S(2)}) collective-permute-start(f32[1,704,256]{2,1,0:T(8,128)} %get-tuple-element.208), channel_id=1, source_target_pairs={{0,3},{1,2},{2,1},{3,0},{4,7},{5,6},{6,5},{7,4}} | collective-permute-start | bytes 2162696 | tf_op jit(solution)/shard_map/ppermute | solution.py:705
  592.4 71.4 %collective-permute-start.18 = (f32[1,704,256]{2,1,0:T(8,128)S(1)}, f32[1,704,256]{2,1,0:T(8,128)S(1)}, u32[]{:S(2)}, u32[]{:S(2)}) collective-permute-start(f32[1,704,256]{2,1,0:T(8,128)S(1)} %copy-done.58), channel_id=1, source_target_pairs={{0,5},{1,4},{2,7},{3,6},{4,1},{5,0},{6,3},{7,2}} | collective-permute-start | bytes 2162696 | tf_op jit(solution)/shard_map/ppermute | solution.py:705
  619.1 71.8 %collective-permute-start.19 = (f32[1,704,256]{2,1,0:T(8,128)S(1)}, f32[1,704,256]{2,1,0:T(8,128)S(1)}, u32[]{:S(2)}, u32[]{:S(2)}) collective-permute-start(f32[1,704,256]{2,1,0:T(8,128)S(1)} %copy-done.57), channel_id=1, source_target_pairs={{0,7},{1,6},{2,5},{3,4},{4,3},{5,2},{6,1},{7,0}} | collective-permute-start | bytes 2162696 | tf_op jit(solution)/shard_map/ppermute | solution.py:705
  623.9 67.0 %collective-permute-start.20 = (f32[1,704,256]{2,1,0:T(8,128)S(1)}, f32[1,704,256]{2,1,0:T(8,128)S(1)}, u32[]{:S(2)}, u32[]{:S(2)}) collective-permute-start(f32[1,704,256]{2,1,0:T(8,128)S(1)} %copy-done.56), channel_id=1, source_target_pairs={{0,1},{1,0},{2,3},{3,2},{4,5},{5,4},{6,7},{7,6}} | collective-permute-start | bytes 2162696 | tf_op jit(solution)/shard_map/ppermute | solution.py:705
  641.4 105.8 %collective-permute-start.21 = (f32[1,704,256]{2,1,0:T(8,128)}, f32[1,704,256]{2,1,0:T(8,128)}, u32[]{:S(2)}, u32[]{:S(2)}) collective-permute-start(f32[1,704,256]{2,1,0:T(8,128)} %get-tuple-element.233), channel_id=1, source_target_pairs={{0,2},{1,3},{2,0},{3,1},{4,6},{5,7},{6,4},{7,5}} | collective-permute-start | bytes 2162696 | tf_op jit(solution)/shard_map/ppermute | solution.py:705
  660.1 89.4 %collective-permute-start.22 = (f32[1,704,256]{2,1,0:T(8,128)}, f32[1,704,256]{2,1,0:T(8,128)}, u32[]{:S(2)}, u32[]{:S(2)}) collective-permute-start(f32[1,704,256]{2,1,0:T(8,128)} %get-tuple-element.234), channel_id=1, source_target_pairs={{0,4},{1,5},{2,6},{3,7},{4,0},{5,1},{6,2},{7,3}} | collective-permute-start | bytes 2162696 | tf_op jit(solution)/shard_map/ppermute | solution.py:705
  740.6 69.9 %all-to-all-start.2 = ((bf16[8,256,256]{2,1,0:T(8,128)(2,1)}), bf16[8,256,256]{2,1,0:T(8,128)(2,1)}, u32[]{:S(2)}, u32[]{:S(2)}) async-start(bf16[8,256,256]{2,1,0:T(8,128)(2,1)} %bitcast.65), calls=%async_computation.3 | async-start | bytes 2097152 | tf_op jit(solution)/shard_map/all_to_all | solution.py:716
  747.2 58.0 %collective-permute-start.26 = (f32[1,704,256]{2,1,0:T(8,128)}, f32[1,704,256]{2,1,0:T(8,128)}, u32[]{:S(2)}, u32[]{:S(2)}) collective-permute-start(f32[1,704,256]{2,1,0:T(8,128)} %get-tuple-element.246), channel_id=1, source_target_pairs={{0,7},{1,6},{2,5},{3,4},{4,3},{5,2},{6,1},{7,0}} | collective-permute-start | bytes 2162696 | tf_op jit(solution)/shard_map/ppermute | solution.py:705
  749.5 55.7 %collective-permute-start.27 = (f32[1,704,256]{2,1,0:T(8,128)}, f32[1,704,256]{2,1,0:T(8,128)}, u32[]{:S(2)}, u32[]{:S(2)}) collective-permute-start(f32[1,704,256]{2,1,0:T(8,128)} %get-tuple-element.247), channel_id=1, source_target_pairs={{0,1},{1,0},{2,3},{3,2},{4,5},{5,4},{6,7},{7,6}} | collective-permute-start | bytes 2162696 | tf_op jit(solution)/shard_map/ppermute | solution.py:705
  (78 other events, 1797.4 us)
Sparse Core Ops, SparseCore 0:
  9.9 68.5 all-gather.4
  80.3 48.6 all-gather.6
  130.8 88.8 all-gather.8
  318.0 135.0 reduce-scatter.1
  587.7 137.0 all-gather.10
